TPU v7x, 32 devices: a 4x2x2 block of a 4x4x8 slice. The times are simulated.
32 devices in a mesh: dp: 4 (over y, z), ep: 8 (over x, core).
Axes of the slice: x: 4, y: 2, z: 2, core: 2. Of those that a mesh axis runs over, the one named last changes fastest.
The devices are a block of a 4x4x8 slice.
Arguments:
- tokens: bfloat16 [6144, 2048], P(('dp', 'ep')), parts along dimension 0
- topk_idx: int32 [6144, 6], P(('dp', 'ep')), parts along dimension 0
- topk_w: float32 [6144, 6], P(('dp', 'ep')), parts along dimension 0
- w_up: bfloat16 [8, 9, 2048, 1408], P('ep')
- w_down: bfloat16 [8, 9, 1408, 2048], P('ep')
- slot_expert: int32 [8, 9], replicated
Outputs:
- output: bfloat16 [6144, 2048], P(('dp', 'ep')), parts along dimension 0
There are 4 independent parts. A program takes and returns all parts, laid end to end along the dimension named above; an argument that names none is the same for every part.
All inputs are finite; a program needn't handle non-finite values.
Results may differ from a plain program's by a relative error of at most 0.00137.
Values are sent between devices in bfloat16 or wider.
A program may use at most 768 MiB of HBM per device.

v0:
```python
import jax
import jax.numpy as jnp
from jax import lax
from jax.sharding import PartitionSpec as P

MAX_COPIES = 4


def slot_bound(n_tok, n_top, n_dev, n_slot):
    base_load = (n_tok * n_top) // (n_dev * n_slot)
    return base_load + base_load // 2 + 1


def route_pairs(topk_idx, slot_expert, capacity):
    n_dev, n_slot = slot_expert.shape
    n_exp = n_dev * (n_slot - 1)
    n_top = topk_idx.shape[1]
    table_flat = slot_expert.reshape(-1)
    slot_ids = jnp.arange(n_dev * n_slot, dtype=jnp.int32)
    same_exp = table_flat[:, None] == table_flat[None, :]
    earlier = slot_ids[None, :] < slot_ids[:, None]
    copy_rank = jnp.sum(same_exp & earlier, axis=1, dtype=jnp.int32)
    exp_copies = jax.ops.segment_sum(jnp.ones_like(table_flat), table_flat, num_segments=n_exp)
    slot_of = jnp.zeros((n_exp, MAX_COPIES), jnp.int32).at[table_flat, copy_rank].set(slot_ids)
    flat_exp = topk_idx.reshape(-1)
    onehot = (flat_exp[:, None] == jnp.arange(n_exp, dtype=jnp.int32)[None, :]).astype(jnp.int32)
    pair_rank = jnp.sum((jnp.cumsum(onehot, axis=0) - onehot) * onehot, axis=1)
    pair_copies = exp_copies[flat_exp]
    slot_flat = slot_of[flat_exp, pair_rank % pair_copies]
    buf_row = pair_rank // pair_copies
    pair_pos = ((slot_flat % n_slot) * n_dev + slot_flat // n_slot) * capacity + buf_row
    pair_tok = jnp.arange(flat_exp.shape[0], dtype=jnp.int32) // n_top
    buf_tok = jnp.zeros((n_slot * n_dev * capacity,), jnp.int32).at[pair_pos].set(pair_tok)
    return pair_pos, buf_tok


def expert_ffn(recv_buf, up_local, down_local):
    pre_act = jnp.einsum('spcm,smf->spcf', recv_buf, up_local, preferred_element_type=jnp.float32)
    hidden = jax.nn.gelu(pre_act, approximate=True).astype(jnp.bfloat16)
    return jnp.einsum('spcf,sfm->spcm', hidden, down_local, preferred_element_type=jnp.float32).astype(jnp.bfloat16)


def solution(mesh):
    def group_layer(tokens, topk_idx, topk_w, w_up, w_down, slot_expert):
        n_tok, d_model = tokens.shape
        n_top = topk_idx.shape[1]
        n_dev, n_slot = slot_expert.shape
        capacity = slot_bound(n_tok, n_top, n_dev, n_slot)
        pair_pos, buf_tok = route_pairs(topk_idx, slot_expert, capacity)
        send_buf = tokens[buf_tok].reshape(n_slot, n_dev, capacity, d_model)
        recv_buf = lax.all_to_all(send_buf, 'ep', 1, 1, tiled=True)
        expert_out = expert_ffn(recv_buf, w_up[0], w_down[0])
        back_buf = lax.all_to_all(expert_out, 'ep', 1, 1, tiled=True)
        pair_out = back_buf.reshape(-1, d_model)[pair_pos].reshape(n_tok, n_top, d_model)
        mixed_out = jnp.sum(pair_out.astype(jnp.float32) * topk_w[:, :, None], axis=1)
        return mixed_out.astype(jnp.bfloat16)

    row_spec = P(('dp', 'ep'), None)
    weight_spec = P('ep', None, None, None)
    return jax.shard_map(group_layer, mesh=mesh, in_specs=(row_spec, row_spec, row_spec, weight_spec, weight_spec, P(None, None)), out_specs=row_spec, check_vma=False)
```

profile of v0, /device:TPU:81, one launch (start us, length us, event | category | flops | bytes accessed | tf_op | source)
XLA Modules:
  0.0 457.9 jit_solution(17501045087045686452)
XLA Ops:
  0.0 0.0 copy-start
  0.0 0.8 eq.53
  0.8 1.0 scatter_custom_fusion.1
  1.9 0.7 fusion.42
  2.6 0.7 fusion.43
  3.3 0.7 fusion.40
  4.0 0.7 fusion.41
  4.8 0.8 copy.24
  5.6 0.1 reshape.255
  5.7 0.1 eq.61
  5.9 0.1 eq.57
  6.0 0.2 convert_reduce_fusion
  6.2 0.8 reshape.254
  6.9 4.3 fusion.26
  11.3 0.8 compare_reduce_fusion.56
  12.2 18.1 %reduce-window.6 = s32[64,9,128]{2,1,0:T(8,128)S(1)} reduce-window(s32[64,9,128]{2,1,0:T(8,128)S(1)} %fusion.18, s32[]{:T(128)} %constant.22.clone.1), window={size=1x1x128 pad=0_0x0_0x127_0}, to_apply=%region_2.0 | reduce-window | flops 9363456 | bytes 589828 | tf_op jit(solution)/shard_map/reduce-window
  30.3 0.2 slice.81
  30.5 0.3 copy.27
  30.8 0.1 copy.28
  30.9 0.2 broadcast_add_fusion
  31.1 0.1 fusion.21
  31.3 35.6 %select_select_fusion = s32[1152]{0:T(1024)S(1)} fusion(pred[1152]{0:T(1024)(128)(4,1)S(1)} %get-tuple-element.61, pred[1152]{0:T(1024)(128)(4,1)S(1)} %get-tuple-element.60, pred[1152]{0:T(1024)(128)(4,1)S(1)} %get-tuple-element.59, pred[1152]{0:T(1024)(128)(4,1)S(1)} %get-tuple-element.58, pred[1152]{0:T(1024)(128)(4,1)S(1)} %get-tuple-element.57, ...), kind=kLoop, calls=%fused_computation.113 | loop fusion | flops 65664 | bytes 75108 | tf_op jit(solution)/shard_map/gather | solution.py:28
  66.9 0.4 fusion.33
  67.4 4.2 scatter_fusion
  71.6 9.5 %gather_fusion = s32[1152]{0:T(1024)S(1)} fusion(s32[64,4]{0,1:T(4,128)S(1)} %scatter_fusion, s32[1152]{0:T(1024)S(1)} %fusion.33), kind=kCustom, calls=%fused_computation | custom fusion | bytes 18432 | tf_op jit(solution)/shard_map/gather | solution.py:29
  81.2 0.4 fusion.27
  81.6 6.4 %scatter_custom_fusion.2 = s32[1800]{0:T(1024)S(1)} fusion(s32[1152]{0:T(1024)S(1)} %fusion.27, s32[1152]{0:T(1024)S(1)} %add_select_fusion, s32[]{:T(128)} %constant.22.clone.1), kind=kCustom, calls=%fused_computation.126 | custom fusion | bytes 7204 | tf_op jit(solution)/shard_map/scatter | solution.py:33
  88.1 0.0 copy-done
  88.1 8.5 %gather_fusion.1 = bf16[1800,2048]{1,0:T(8,128)(2,1)} fusion(bf16[192,2048]{1,0:T(8,128)(2,1)S(1)} %copy-done, s32[2048]{0:T(1024)S(1)} %pad_clamp_fusion.1), kind=kCustom, calls=%fused_computation.1 | custom fusion | bytes 14752800 | tf_op jit(solution)/shard_map/gather | solution.py:50
  96.7 10.7 %reshape.257 = bf16[9,8,25,2048]{3,2,1,0:T(8,128)(2,1)} reshape(bf16[1800,2048]{1,0:T(8,128)(2,1)} %gather_fusion.1) | data formatting | bytes 14745600 | tf_op jit(solution)/shard_map/reshape | solution.py:50
  107.3 9.3 %copy.29 = bf16[9,8,25,2048]{3,2,0,1:T(8,128)(2,1)} copy(bf16[9,8,25,2048]{3,2,1,0:T(8,128)(2,1)} %reshape.257) | data formatting | bytes 14745600 | tf_op jit(solution)/shard_map/reshape | solution.py:50
  116.6 112.6 %all_to_all.10 = bf16[9,8,25,2048]{3,2,0,1:T(8,128)(2,1)} all-to-all(bf16[9,8,25,2048]{3,2,0,1:T(8,128)(2,1)} %copy.29), channel_id=1, replica_groups=mesh['dp'=4,'ep'=8] {'ep'}, dimensions={1} | all-to-all | bytes 14745600 | tf_op jit(solution)/shard_map/all_to_all | solution.py:51
  229.2 27.8 %fusion.11 = bf16[9,8,25,1408]{3,2,1,0:T(8,128)(2,1)} fusion(bf16[1,9,2048,1408]{3,2,1,0:T(8,128)(2,1)} %param.9, bf16[9,8,25,2048]{3,2,0,1:T(8,128)(2,1)} %all_to_all.10), kind=kOutput, calls=%fused_computation.18 | convolution fusion | flops 10403712000 | bytes 64346112 | tf_op jit(solution)/shard_map/spcm,smf->spcf/dot_general | solution.py:38
  257.1 26.0 %fusion.15 = bf16[9,8,25,2048]{3,2,1,0:T(8,128)(2,1)} fusion(bf16[9,8,25,1408]{3,2,1,0:T(8,128)(2,1)} %fusion.11, bf16[1,9,1408,2048]{3,2,1,0:T(8,128)(2,1)} %param.10), kind=kOutput, calls=%fused_computation.21 | convolution fusion | flops 10384588800 | bytes 64346112 | tf_op jit(solution)/shard_map/spcf,sfm->spcm/dot_general | solution.py:40
  283.1 9.3 %copy.31 = bf16[9,8,25,2048]{3,2,0,1:T(8,128)(2,1)} copy(bf16[9,8,25,2048]{3,2,1,0:T(8,128)(2,1)} %fusion.15) | data formatting | bytes 14745600 | tf_op jit(solution)/shard_map/convert_element_type | solution.py:40
  292.3 0.0 copy-start.2
  292.3 6.2 %all-to-all-start.1 = ((bf16[9,8,25,2048]{3,2,0,1:T(8,128)(2,1)}), bf16[9,8,25,2048]{3,2,0,1:T(8,128)(2,1)}, u32[]{:S(2)}, u32[]{:S(2)}) async-start(bf16[9,8,25,2048]{3,2,0,1:T(8,128)(2,1)} %copy.31), calls=%async_computation.1 | async-start | bytes 18874368 | tf_op jit(solution)/shard_map/all_to_all | solution.py:53
  298.5 0.0 copy-done.2
  298.5 0.1 copy.33
  298.6 104.7 %all-to-all-done.1 = bf16[9,8,25,2048]{3,2,0,1:T(8,128)(2,1)} async-done(((bf16[9,8,25,2048]{3,2,0,1:T(8,128)(2,1)}), bf16[9,8,25,2048]{3,2,0,1:T(8,128)(2,1)}, u32[]{:S(2)}, u32[]{:S(2)}) %all-to-all-start.1) | async-done | bytes 7372832 | tf_op jit(solution)/shard_map/all_to_all | solution.py:53
  403.3 9.3 %copy.32 = bf16[9,8,25,2048]{3,2,1,0:T(8,128)(2,1)} copy(bf16[9,8,25,2048]{3,2,0,1:T(8,128)(2,1)} %all-to-all-done.1) | data formatting | bytes 14745600 | tf_op jit(solution)/shard_map/all_to_all | solution.py:53
  412.6 10.9 %reshape.258 = bf16[1800,2048]{1,0:T(8,128)(2,1)} reshape(bf16[9,8,25,2048]{3,2,1,0:T(8,128)(2,1)} %copy.32) | data formatting | bytes 14745600 | tf_op jit(solution)/shard_map/reshape | solution.py:54
  423.5 0.0 copy-start.1
  423.5 14.8 %gather_fusion.2 = bf16[1152,2048]{1,0:T(8,128)(2,1)} fusion(bf16[1800,2048]{1,0:T(8,128)(2,1)} %reshape.258, s32[2048]{0:T(1024)S(1)} %pad_clamp_fusion), kind=kCustom, calls=%fused_computation.2 | custom fusion | bytes 9441792 | tf_op jit(solution)/shard_map/gather | solution.py:54
  438.3 9.1 %reshape.259 = f32[192,6,2048]{2,1,0:T(8,128)} reshape(bf16[1152,2048]{1,0:T(8,128)(2,1)} %gather_fusion.2) | data formatting | bytes 14155776 | tf_op jit(solution)/shard_map/convert_element_type | solution.py:55
  447.4 10.5 %multiply_reduce_fusion = bf16[192,2048]{1,0:T(8,128)(2,1)} fusion(f32[192,6,2048]{2,1,0:T(8,128)} %reshape.259, f32[192,6]{1,0:T(8,128)S(1)} %copy.33), kind=kLoop, calls=%fused_computation.19 | loop fusion | flops 4325376 | bytes 10228224 | tf_op jit(solution)/shard_map/reduce_sum | solution.py:55
  457.9 0.0 copy-done.1
  (12 shorter events, 0.1 us)
Async XLA Ops:
  0.0 88.1 %copy-start = (bf16[192,2048]{1,0:T(8,128)(2,1)S(1)}, bf16[192,2048]{1,0:T(8,128)(2,1)}, u32[]{:S(2)}) copy-start(bf16[192,2048]{1,0:T(8,128)(2,1)} %param.6) | copy-start | bytes 2359300
  292.3 6.2 %copy-start.2 = (f32[192,6]{0,1:T(8,128)S(1)}, f32[192,6]{0,1:T(8,128)}, u32[]{:S(2)}) copy-start(f32[192,6]{0,1:T(8,128)} %param.8) | copy-start | bytes 13828
  292.3 111.0 %all-to-all-start.1 = ((bf16[9,8,25,2048]{3,2,0,1:T(8,128)(2,1)}), bf16[9,8,25,2048]{3,2,0,1:T(8,128)(2,1)}, u32[]{:S(2)}, u32[]{:S(2)}) async-start(bf16[9,8,25,2048]{3,2,0,1:T(8,128)(2,1)} %copy.31), calls=%async_computation.1 | async-start | bytes 18874368 | tf_op jit(solution)/shard_map/all_to_all | solution.py:53
  423.5 34.3 %copy-start.1 = (bf16[192,2048]{1,0:T(8,128)(2,1)S(1)}, bf16[192,2048]{1,0:T(8,128)(2,1)}, u32[]{:S(2)}) copy-start(bf16[192,2048]{1,0:T(8,128)(2,1)} %param.6) | copy-start | bytes 2359300
where the time goes:
time: 460 us; the launch traced here: 458 us
  blocking collectives  113 us (25%)
  local copies, waits for them, and re-layouts  108 us (23%)
  waiting for transfers between devices  105 us (23%)
  other arithmetic  72 us (16%)
  matrix products  53.8 us (12%)
  starting transfers between devices  6.17 us (1%)
    all_to_all x1, blocking collectives, group_layer(): recv_buf = lax.all_to_all(send_buf, 'ep', 1, 1, tiled=True)  113 us
    all_to_all x1, waiting for transfers between devices, group_layer(): back_buf = lax.all_to_all(expert_out, 'ep', 1, 1, tiled=True)  105 us
    gather x3, other arithmetic, route_pairs(): pair_copies = exp_copies[flat_exp]  40.8 us
    dot_general x1, matrix products, expert_ffn(): jnp.einsum('spcm,smf->spcf', recv_buf, up_local, preferred_element_type=j...  27.8 us
    dot_general x1, matrix products, expert_ffn(): jnp.einsum('spcf,sfm->spcm', hidden, down_local, preferred_element_type=j...  26 us
    reshape x2, local copies, waits for them, and re-layouts, group_layer(): send_buf = tokens[buf_tok].reshape(n_slot, n_dev, capacity, d_model)  19.9 us
    another operation x3, other arithmetic  18.4 us
    gather x1, local copies, waits for them, and re-layouts, group_layer(): back_buf.reshape(-1, d_model)[pair_pos].reshape(n_tok, n_top, d_model)  14.8 us
  transfers between devices with their start and end apart: 1, of which 1 were waited for; matrix products, arithmetic and copies ran while one was open for 0% of the time, Pallas kernels for 0%

commit v1 on v0

v1 whole, which is shorter than its diff:
```python
import functools

import jax
import jax.numpy as jnp
from jax import lax
from jax.experimental import pallas as pl
from jax.experimental.pallas import tpu as pltpu
from jax.sharding import PartitionSpec as P

MESH = pl.DeviceIdType.MESH
F32 = jnp.float32
BF16 = jnp.bfloat16
LANES = 128
CHIPS = 4
AHEAD = 2
STAGES = 4


def slot_bound(n_tok, n_top, n_dev, n_slot):
    base_load = (n_tok * n_top) // (n_dev * n_slot)
    return base_load + base_load // 2 + 1


def round_up(n, m):
    return -(-n // m) * m


def gelu(v):
    return v * (0.5 + 0.5 * jnp.tanh(v * (0.7978845608028654 + (0.7978845608028654 * 0.044715) * (v * v))))


def dot(a, b):
    return lax.dot_general(a, b, (((1,), (0,)), ((), ())), preferred_element_type=F32)


def moe_kernel(cfg, x_ref, meta_ref, ecol_ref, trk_ref, wup_ref, wdn_ref, y_ref,
               xall, meta_all, g_buf, c_buf, xg, acc, h_buf, o_buf, wu, wd, sib_in, far_in, dir_in, mrg_in,
               meta_ss, meta_rs, near_ss, near_rs, rel_ss, rel_rs, sib_ss, sib_rs, wu_s, wd_s,
               ps_ss, ps_rs, pf_ss, pf_rs, pd_ss, pd_rs, pm_ss, pm_rs):
    n_tok, d_model, d_ff, n_slot, cap, kb_w, cb_w, n_top, d_mid = (
        cfg[k] for k in ("n_tok", "d_model", "d_ff", "n_slot", "cap", "kb_w", "cb_w", "n_top", "d_mid"))
    n_kb, n_cb = d_model // kb_w, d_model // cb_w
    n_src = 2 * CHIPS
    half = n_tok // 2
    nu, nd = wu.shape[0], wd.shape[0]
    me = lax.axis_index("ep")
    chip, core = me // 2, me % 2

    def dev(d_chip, d_core=0):
        return {"ep": ((chip + d_chip) % CHIPS) * 2 + (core + d_core) % 2}

    right, left, sib = dev(1), dev(CHIPS - 1), dev(0, 1)

    def rcopy(src, dst, ss, rs, to):
        return pltpu.make_async_remote_copy(src_ref=src, dst_ref=dst, send_sem=ss, recv_sem=rs, device_id=to, device_id_type=MESH)

    def up_load(i):
        return pltpu.make_async_copy(
            wup_ref.at[0, i % n_slot, pl.ds(pl.multiple_of((i // n_slot) * kb_w, kb_w), kb_w), :], wu.at[i % nu], wu_s.at[i % nu])

    def down_load(i):
        return pltpu.make_async_copy(
            wdn_ref.at[0, i % n_slot, :, pl.ds(pl.multiple_of((i // n_slot) * cb_w, cb_w), cb_w)], wd.at[i % nd], wd_s.at[i % nd])

    for i in range(nu):
        up_load(i).start()

    barrier = pltpu.get_barrier_semaphore()
    peers = [(dx, dc) for dx in range(CHIPS) for dc in range(2) if dx or dc]
    for dx, dc in peers:
        pl.semaphore_signal(barrier, inc=1, device_id=dev(dx, dc), device_id_type=MESH)
    pl.semaphore_wait(barrier, len(peers))

    sends = []

    def go(copy):
        copy.start()
        sends.append(copy)

    def own(kb):
        return x_ref.at[:, pl.ds(kb * kb_w, kb_w)]

    near = [(rcopy(own(kb), xall.at[2 * (CHIPS - 1), kb], near_ss.at[kb, 0], near_rs.at[kb, 0], right),
             rcopy(own(kb), xall.at[2, kb], near_ss.at[kb, 1], near_rs.at[kb, 1], left)) for kb in range(n_kb)]
    lo, hi = pl.ds(0, half), pl.ds(half, n_tok - half)
    relay = [(rcopy(xall.at[2 * (CHIPS - 1), kb, lo], xall.at[4, kb, lo], rel_ss.at[kb, 0], rel_rs.at[kb, 0], right),
              rcopy(xall.at[2, kb, hi], xall.at[4, kb, hi], rel_ss.at[kb, 1], rel_rs.at[kb, 1], left)) for kb in range(n_kb)]
    across = [[rcopy(own(kb) if off == 0 else xall.at[2 * off, kb], xall.at[2 * off + 1, kb],
                     sib_ss.at[kb, off], sib_rs.at[kb, off], sib) for off in range(CHIPS)] for kb in range(n_kb)]
    metas = []
    for n, (dx, dc) in enumerate(peers):
        metas.append(rcopy(meta_ref, meta_all.at[2 * ((CHIPS - dx) % CHIPS) + dc], meta_ss.at[n], meta_rs.at[n], dev(dx, dc)))

    for m in metas:
        go(m)
    for kb in range(min(AHEAD, n_kb)):
        go(near[kb][0])
        go(near[kb][1])
    for kb in range(n_kb):
        go(across[kb][0])

    meta_all[0] = meta_ref[...]
    for kb in range(n_kb):
        xall[0, kb] = x_ref[:, kb * kb_w:(kb + 1) * kb_w]

    def stage_near(kb):
        for c, r, off in ((near[kb][0], relay[kb][0], CHIPS - 1), (near[kb][1], relay[kb][1], 1)):
            c.wait_recv()
            go(r)
            go(across[kb][off])
        if kb + AHEAD < n_kb:
            go(near[kb + AHEAD][0])
            go(near[kb + AHEAD][1])

    for m in metas:
        m.wait_recv()
    lane_tok = meta_ref.shape[1]
    earlier = (lax.broadcasted_iota(jnp.int32, (lane_tok, lane_tok), 0)
               < lax.broadcasted_iota(jnp.int32, (lane_tok, lane_tok), 1)).astype(F32).astype(BF16)
    e_col = ecol_ref[:, 0:1]
    rows_src = n_slot * cap
    rows_pad = round_up(rows_src, LANES)

    def route(j, carry):
        m = meta_all[j]
        has = jnp.zeros((ecol_ref.shape[0], lane_tok), F32)
        gate = jnp.zeros((ecol_ref.shape[0], lane_tok), F32)
        for q in range(n_top):
            hit = m[q:q + 1, :] == e_col
            has = jnp.where(hit, 1.0, has)
            gate = jnp.where(hit, m[8 + q:9 + q, :], gate)
        rank = jnp.where(has > 0.0, dot(has.astype(BF16), earlier), -1.0)
        parts = []
        for s in range(n_slot):
            hit = rank[s:s + 1, :] == trk_ref[s * cap:(s + 1) * cap, 0:1]
            g_buf[j, s * cap:(s + 1) * cap, :] = jnp.where(hit, 1.0, 0.0)[:, :n_tok].astype(BF16)
            parts.append(jnp.where(hit, gate[s:s + 1, :], 0.0))
        if rows_pad > rows_src:
            parts.append(jnp.zeros((rows_pad - rows_src, lane_tok), F32))
        gates = jnp.transpose(jnp.concatenate(parts, axis=0))[:n_tok, :rows_src]
        for n in range(3):
            term = gates.astype(BF16)
            c_buf[j, n * n_tok:(n + 1) * n_tok, :] = term
            gates = gates - term.astype(F32)
        return carry

    lax.fori_loop(0, n_src, route, 0)

    chunks = [(n, min(2 * LANES, d_ff - n)) for n in range(0, d_ff, 2 * LANES)]
    n_mid = d_ff // LANES

    stage_near(0)
    for kb in range(n_kb):
        if kb + 1 < n_kb:
            stage_near(kb + 1)
        relay[kb][0].wait_recv()
        relay[kb][1].wait_recv()
        go(across[kb][2])
        for c in across[kb]:
            c.wait_recv()

        def gather(j, carry, kb=kb):
            rows = dot(g_buf[j], xall[j, kb]).astype(BF16)
            for s in range(n_slot):
                xg[s, pl.ds(pl.multiple_of(j * cap, cap), cap), :] = rows[s * cap:(s + 1) * cap]
            return carry

        lax.fori_loop(0, n_src, gather, 0)

        def up(s, carry, kb=kb):
            i = kb * n_slot + s
            up_load(i).wait()
            for n0, nw in chunks:
                v = dot(xg[s], wu[i % nu, :, n0:n0 + nw])
                for n in range(0, nw, LANES):
                    q = s * n_mid + (n0 + n) // LANES
                    part = v[:, n:n + LANES]
                    if kb > 0:
                        part = acc[q, :d_mid, :] + part
                    if kb < n_kb - 1:
                        acc[q, :d_mid, :] = part
                    else:
                        h_buf[s, :, n0 + n:n0 + n + LANES] = gelu(part).astype(BF16)

            @pl.when(i + nu < n_kb * n_slot)
            def _():
                up_load(i + nu).start()
            return carry

        lax.fori_loop(0, n_slot, up, 0)
        if kb == 0:
            for i in range(nd):
                down_load(i).start()

    def mine(cb, off, h):
        return (cb * CHIPS + off) * 2 + h

    def staged(cb, off, h):
        return n_cb * CHIPS * 2 + ((cb % STAGES) * CHIPS + off) * 2 + h

    tok = pl.ds(0, n_tok)
    to_sib = [[rcopy(acc.at[pl.ds(staged(cb, off, 0), 2), tok], sib_in.at[cb, off], ps_ss.at[cb, off], ps_rs.at[cb, off], sib)
               for off in range(CHIPS)] for cb in range(n_cb)]
    to_far = [(rcopy(acc.at[mine(cb, 2, 0), tok], far_in.at[cb, 0], pf_ss.at[cb, 0], pf_rs.at[cb, 0], right),
               rcopy(acc.at[mine(cb, 2, 1), tok], far_in.at[cb, 1], pf_ss.at[cb, 1], pf_rs.at[cb, 1], left)) for cb in range(n_cb)]
    to_dir = [(rcopy(acc.at[mine(cb, 1, 1), tok], dir_in.at[cb, 0], pd_ss.at[cb, 0], pd_rs.at[cb, 0], right),
               rcopy(acc.at[mine(cb, 3, 0), tok], dir_in.at[cb, 1], pd_ss.at[cb, 1], pd_rs.at[cb, 1], left)) for cb in range(n_cb)]
    to_mrg = [(rcopy(far_in.at[cb, 0], mrg_in.at[cb, 0], pm_ss.at[cb, 0], pm_rs.at[cb, 0], right),
               rcopy(far_in.at[cb, 1], mrg_in.at[cb, 1], pm_ss.at[cb, 1], pm_rs.at[cb, 1], left)) for cb in range(n_cb)]
    waited = set()

    def merge(cb):
        to_far[cb][0].wait_recv()
        far_in[cb, 0] = far_in[cb, 0] + acc[mine(cb, 1, 0), :n_tok, :]
        go(to_mrg[cb][0])
        to_far[cb][1].wait_recv()
        far_in[cb, 1] = far_in[cb, 1] + acc[mine(cb, 3, 1), :n_tok, :]
        go(to_mrg[cb][1])

    def finish(cb):
        for h in range(2):
            to_mrg[cb][h].wait_recv()
            to_dir[cb][1 - h].wait_recv()
            total = acc[mine(cb, 0, h), :n_tok, :] + mrg_in[cb, h] + dir_in[cb, 1 - h]
            y_ref[:, cb * cb_w + h * LANES:cb * cb_w + (h + 1) * LANES] = total.astype(BF16)

    for cb in range(n_cb):
        def down(s, carry, cb=cb):
            i = cb * n_slot + s
            down_load(i).wait()
            out = dot(h_buf[s], wd[i % nd]).astype(BF16)
            for j in range(n_src):
                o_buf[j, pl.ds(pl.multiple_of(s * cap, cap), cap), :] = out[j * cap:(j + 1) * cap]

            @pl.when(i + nd < n_cb * n_slot)
            def _():
                down_load(i + nd).start()
            return carry

        lax.fori_loop(0, n_slot, down, 0)
        if cb >= STAGES:
            for off in range(CHIPS):
                to_sib[cb - STAGES][off].wait_send()
                waited.add(id(to_sib[cb - STAGES][off]))

        def combine(off, carry, dc, first):
            v = dot(c_buf[2 * off + dc], o_buf[2 * off + dc])
            v = (v[2 * n_tok:] + v[n_tok:2 * n_tok]) + v[:n_tok]
            acc[first + 2 * off, :n_tok, :] = v[:, :LANES]
            acc[first + 2 * off + 1, :n_tok, :] = v[:, LANES:]
            return carry

        lax.fori_loop(0, CHIPS, functools.partial(combine, dc=1, first=staged(cb, 0, 0)), 0)
        for off in (2, 1, 3, 0):
            go(to_sib[cb][off])
        lax.fori_loop(0, CHIPS, functools.partial(combine, dc=0, first=mine(cb, 0, 0)), 0)
        for off in (2, 1, 3, 0):
            to_sib[cb][off].wait_recv()
            for h in range(2):
                q = mine(cb, off, h)
                acc[q, :n_tok, :] = acc[q, :n_tok, :] + sib_in[cb, off, h]
            if off == 2:
                go(to_far[cb][0])
                go(to_far[cb][1])
            elif off:
                go(to_dir[cb][0 if off == 1 else 1])
        if cb >= 1:
            merge(cb - 1)
        if cb >= 2:
            finish(cb - 2)
    merge(n_cb - 1)
    for cb in range(max(0, n_cb - 2), n_cb):
        finish(cb)
    for c in sends:
        if id(c) not in waited:
            c.wait_send()


def solution(mesh):
    assert mesh.shape["ep"] == 2 * CHIPS

    def group_layer(tokens, topk_idx, topk_w, w_up, w_down, slot_expert):
        n_tok, d_model = tokens.shape
        n_top = topk_idx.shape[1]
        n_dev, n_slot = slot_expert.shape
        d_ff = w_up.shape[-1]
        bound = slot_bound(n_tok, n_top, n_dev, n_slot)
        cap = round_up(bound, 16)
        kb_w, cb_w = 2 * LANES, 2 * LANES
        n_kb, n_cb = d_model // kb_w, d_model // cb_w
        n_src = n_dev
        lane_tok = round_up(n_tok, LANES)

        me = lax.axis_index("ep")
        flat = slot_expert.reshape(-1)
        n_all = flat.shape[0]
        same = flat[:, None] == flat[None, :]
        ids = jnp.arange(n_all, dtype=jnp.int32)
        copy_rank = jnp.sum(same & (ids[None, :] < ids[:, None]), axis=1, dtype=jnp.int32)
        copies = jnp.sum(same, axis=1, dtype=jnp.int32)
        my_exp = lax.dynamic_slice_in_dim(flat, me * n_slot, n_slot)
        my_rank = lax.dynamic_slice_in_dim(copy_rank, me * n_slot, n_slot)
        my_copies = lax.dynamic_slice_in_dim(copies, me * n_slot, n_slot)
        r = jnp.arange(cap, dtype=jnp.int32)[None, :]
        trk = jnp.where(r < bound, r * my_copies[:, None] + my_rank[:, None], -2).astype(F32).reshape(-1, 1)
        trk = jnp.broadcast_to(trk, (n_slot * cap, LANES))
        ecol = jnp.pad(my_exp.astype(F32), (0, round_up(n_slot, 8) - n_slot), constant_values=-2.0)
        ecol = jnp.broadcast_to(ecol[:, None], (ecol.shape[0], LANES))
        pad = ((0, 8 - n_top), (0, lane_tok - n_tok))
        meta = jnp.concatenate([jnp.pad(topk_idx.astype(F32).T, pad, constant_values=-1.0), jnp.pad(topk_w.T, pad)], axis=0)

        d_mid = n_src * cap
        n_mid = d_ff // LANES
        rows_src = n_slot * cap
        n_acc = max(n_slot * n_mid, (n_cb + STAGES) * CHIPS * 2)
        nu, nd = 6, 16
        cfg = dict(n_tok=n_tok, d_model=d_model, d_ff=d_ff, n_slot=n_slot, cap=cap, kb_w=kb_w, cb_w=cb_w, n_top=n_top, d_mid=d_mid)
        dma = pltpu.SemaphoreType.DMA
        vmem = pl.BlockSpec(memory_space=pltpu.VMEM)
        hbm = pl.BlockSpec(memory_space=pl.ANY)
        return pl.pallas_call(
            functools.partial(moe_kernel, cfg),
            out_shape=jax.ShapeDtypeStruct((n_tok, d_model), BF16),
            in_specs=[vmem, vmem, vmem, vmem, hbm, hbm],
            out_specs=vmem,
            scratch_shapes=[
                pltpu.VMEM((n_src, n_kb, n_tok, kb_w), BF16),
                pltpu.VMEM((n_src,) + meta.shape, F32),
                pltpu.VMEM((n_src, rows_src, n_tok), BF16),
                pltpu.VMEM((n_src, 3 * n_tok, rows_src), BF16),
                pltpu.VMEM((n_slot, d_mid, kb_w), BF16),
                pltpu.VMEM((n_acc, max(d_mid, n_tok), LANES), F32),
                pltpu.VMEM((n_slot, d_mid, d_ff), BF16),
                pltpu.VMEM((n_src, rows_src, cb_w), BF16),
                pltpu.VMEM((nu, kb_w, d_ff), BF16),
                pltpu.VMEM((nd, d_ff, cb_w), BF16),
                pltpu.VMEM((n_cb, CHIPS, 2, n_tok, LANES), F32),
                pltpu.VMEM((n_cb, 2, n_tok, LANES), F32),
                pltpu.VMEM((n_cb, 2, n_tok, LANES), F32),
                pltpu.VMEM((n_cb, 2, n_tok, LANES), F32),
                dma((n_src - 1,)), dma((n_src - 1,)),
                dma((n_kb, 2)), dma((n_kb, 2)), dma((n_kb, 2)), dma((n_kb, 2)),
                dma((n_kb, CHIPS)), dma((n_kb, CHIPS)),
                dma((nu,)), dma((nd,)),
                dma((n_cb, CHIPS)), dma((n_cb, CHIPS)),
                dma((n_cb, 2)), dma((n_cb, 2)), dma((n_cb, 2)), dma((n_cb, 2)), dma((n_cb, 2)), dma((n_cb, 2)),
            ],
            compiler_params=pltpu.CompilerParams(collective_id=0, has_side_effects=True, vmem_limit_bytes=67_000_000),
        )(tokens, meta, ecol, trk, w_up, w_down)

    row_spec = P(('dp', 'ep'), None)
    weight_spec = P('ep', None, None, None)
    return jax.shard_map(group_layer, mesh=mesh, in_specs=(row_spec, row_spec, row_spec, weight_spec, weight_spec, P(None, None)),
                         out_specs=row_spec, check_vma=False)
```

time: 460 us -> 147 us (0.32)
  Pallas kernels: 0 us -> 140 us
  blocking collectives: 113 us -> 0 us
  waiting for transfers between devices: 105 us -> 0 us
  local copies, waits for them, and re-layouts: 108 us -> 4.52 us
  other arithmetic: 72 us -> 2.34 us
  matrix products: 53.8 us -> 0 us
  starting transfers between devices: 6.17 us -> 0 us
    pallas_call x0 -> x1, Pallas kernels: none -> 140 us  [group_layer(): pl.pallas_call(functools.partial(moe_kernel, cfg), out_shape=jax.ShapeDty...]
    all_to_all x1 -> x0, blocking collectives: 113 us -> none  [group_layer(): recv_buf = lax.all_to_all(send_buf, 'ep', 1, 1, tiled=True)]
    all_to_all x1 -> x0, waiting for transfers between devices: 105 us -> none  [group_layer(): back_buf = lax.all_to_all(expert_out, 'ep', 1, 1, tiled=True)]
    dot_general x2 -> x0, matrix products: 53.8 us -> none  [the longest x1 27.8 us: expert_ffn(): jnp.einsum('spcm,smf->spcf', recv_buf, up_local, preferred_element_type=j...]
    gather x5 -> x0, other arithmetic: 40.8 us -> none  [the longest x3 40.8 us: route_pairs(): pair_copies = exp_copies[flat_exp]]
    gather x7 -> x0, local copies, waits for them, and re-layouts: 35.7 us -> none  [the longest x1 14.8 us: group_layer(): back_buf.reshape(-1, d_model)[pair_pos].reshape(n_tok, n_top, d_model)]
    reshape x5 -> x1, local copies, waits for them, and re-layouts: 31.8 us -> 0.76 us  [group_layer(): flat = slot_expert.reshape(-1)]
    another operation x3 -> x0, other arithmetic: 18.4 us -> none
  transfers between devices with their start and end apart: 1 -> 0, of which waited for: 1 -> 0; matrix products, arithmetic and copies ran while one was open for 0% -> 0% of each run, Pallas kernels for 0% -> 0%
where the time goes in v1:
time: 147 us
  Pallas kernels  140 us (95%)
  local copies, waits for them, and re-layouts  4.52 us (3%)
  other arithmetic  2.34 us (2%)
    pallas_call x1, Pallas kernels, group_layer(): pl.pallas_call(functools.partial(moe_kernel, cfg), out_shape=jax.ShapeDty...  140 us

profile of v1, /device:TPU:81, one launch (start us, length us, event | category | flops | bytes accessed | tf_op | source)
XLA Modules:
  0.0 147.0 jit_solution(1866657479984517513)
XLA Ops:
  0.0 0.8 reshape.47
  0.8 0.1 dynamic-slice_convert_fusion
  0.9 0.2 fusion
  1.0 0.1 dynamic_slice.10
  1.1 0.1 dynamic_slice.11
  1.2 0.1 select_convert_fusion
  1.3 0.1 convert_element_type.29
  1.4 0.7 broadcast_in_dim.16.ecol_ref
  2.0 0.7 convert_bitcast_fusion
  2.7 1.3 select_maximum_fusion.meta_ref
  4.0 0.8 broadcast_in_dim.19.trk_ref
  4.8 140.1 %shard_map.64 = bf16[192,2048]{1,0:T(8,128)(2,1)} custom-call(bf16[192,2048]{1,0:T(8,128)(2,1)} %x_ref.1, f32[16,256]{1,0:T(8,128)} %select_maximum_fusion.meta_ref, f32[16,128]{1,0:T(8,128)} %broadcast_in_dim.16.ecol_ref, f32[288,128]{1,0:T(8,128)} %broadcast_in_dim.19.trk_ref, bf16[1,9,2048,1408]{3,2,1,0:T(8,128)(2,1)} %wup_ref.1, ...), custom_call_target="tpu_custom_call" | custom-call | tf_op jit(solution)/shard_map/pallas_call | solution.py:321
  144.9 2.1 %copy.8 = bf16[192,2048]{1,0:T(8,128)(2,1)} copy(bf16[192,2048]{1,0:T(8,128)(2,1)} %shard_map.64) | data formatting | bytes 1572864
  (2 shorter events, 0.0 us)

commit v2 on v1

v2 whole, which is shorter than its diff:
```python
import functools

import jax
import jax.numpy as jnp
from jax import lax
from jax.experimental import pallas as pl
from jax.experimental.pallas import tpu as pltpu
from jax.sharding import PartitionSpec as P

MESH = pl.DeviceIdType.MESH
F32 = jnp.float32
BF16 = jnp.bfloat16
LANES = 128
CHIPS = 4
AHEAD = 2
STAGES = 4
GROUP = 3
LAG = 3


def slot_bound(n_tok, n_top, n_dev, n_slot):
    base_load = (n_tok * n_top) // (n_dev * n_slot)
    return base_load + base_load // 2 + 1


def round_up(n, m):
    return -(-n // m) * m


def gelu(v):
    return v * (0.5 + 0.5 * jnp.tanh(v * (0.7978845608028654 + (0.7978845608028654 * 0.044715) * (v * v))))


def dot(a, b):
    return lax.dot_general(a, b, (((1,), (0,)), ((), ())), preferred_element_type=F32)


def moe_kernel(cfg, x_ref, idx_ref, gate_ref, tab_ref, wup_ref, wdn_ref, y_ref,
               xall, idx_all, gate_all, trk, g_buf, c_buf, xg, acc, h_buf, o_buf, wu, wd, sib_in, far_in, dir_in, mrg_in,
               meta_ss, meta_rs, near_ss, near_rs, rel_ss, rel_rs, sib_ss, sib_rs, wu_s, wd_s,
               ps_ss, ps_rs, pf_ss, pf_rs, pd_ss, pd_rs, pm_ss, pm_rs):
    bound, cap, kb_w, cb_w = (cfg[k] for k in ("bound", "cap", "kb_w", "cb_w"))
    n_tok, d_model = x_ref.shape
    n_top = idx_ref.shape[0]
    n_dev, n_slot = tab_ref.shape
    d_ff = wup_ref.shape[-1]
    d_mid = n_dev * cap
    n_kb, n_cb = d_model // kb_w, d_model // cb_w
    half = n_tok // 2
    me = lax.axis_index("ep")
    chip, core = me // 2, me % 2

    def dev(d_chip, d_core=0):
        return {"ep": ((chip + d_chip) % CHIPS) * 2 + (core + d_core) % 2}

    right, left, sib = dev(1), dev(CHIPS - 1), dev(0, 1)

    def rcopy(src, dst, ss, rs, to):
        return pltpu.make_async_remote_copy(src_ref=src, dst_ref=dst, send_sem=ss, recv_sem=rs, device_id=to, device_id_type=MESH)

    def up_load(kb, s):
        return pltpu.make_async_copy(wup_ref.at[0, s, pl.ds(pl.multiple_of(kb * kb_w, kb_w), kb_w), :], wu.at[s], wu_s.at[s])

    def down_load(cb, s):
        return pltpu.make_async_copy(wdn_ref.at[0, s, :, pl.ds(cb * cb_w, cb_w)], wd.at[s], wd_s.at[s])

    barrier = pltpu.get_barrier_semaphore()
    peers = [(dx, dc) for dx in range(CHIPS) for dc in range(2) if dx or dc]
    for dx, dc in peers:
        pl.semaphore_signal(barrier, inc=1, device_id=dev(dx, dc), device_id_type=MESH)
    for s in range(n_slot):
        up_load(0, s).start()
    pl.semaphore_wait(barrier, len(peers))

    lo, hi = pl.ds(0, half), pl.ds(half, n_tok - half)
    prev = CHIPS - 1

    def own(kb):
        return x_ref.at[:, pl.ds(pl.multiple_of(kb * kb_w, kb_w), kb_w)]

    def near(kb):
        return (rcopy(own(kb), xall.at[2 * prev, kb], near_ss.at[kb, 0], near_rs.at[kb, 0], right),
                rcopy(own(kb), xall.at[2, kb], near_ss.at[kb, 1], near_rs.at[kb, 1], left))

    def relay(kb):
        return (rcopy(xall.at[2 * prev, kb, lo], xall.at[4, kb, lo], rel_ss.at[kb, 0], rel_rs.at[kb, 0], right),
                rcopy(xall.at[2, kb, hi], xall.at[4, kb, hi], rel_ss.at[kb, 1], rel_rs.at[kb, 1], left))

    def across(kb, off):
        return rcopy(xall.at[2 * off, kb] if off else own(kb), xall.at[2 * off + 1, kb], sib_ss.at[kb, off], sib_rs.at[kb, off], sib)

    def start_near(kb):
        for c in near(kb):
            c.start()

    def stage_near(kb):
        for c, r, off in zip(near(kb), relay(kb), (prev, 1)):
            c.wait_recv()
            r.start()
            across(kb, off).start()

    def stage_far(kb):
        for r in relay(kb):
            r.wait_recv()
        across(kb, 2).start()

    metas = []
    for n, (dx, dc) in enumerate(peers):
        place = 2 * ((CHIPS - dx) % CHIPS) + dc
        metas.append(rcopy(idx_ref, idx_all.at[place], meta_ss.at[n, 0], meta_rs.at[n, 0], dev(dx, dc)))
        metas.append(rcopy(gate_ref, gate_all.at[place], meta_ss.at[n, 1], meta_rs.at[n, 1], dev(dx, dc)))
    start_near(0)
    for m in metas:
        m.start()
    for kb in range(1, AHEAD):
        start_near(kb)
    for kb in range(n_kb):
        across(kb, 0).start()
    for s in range(n_slot):
        down_load(0, s).start()

    idx_all[0] = idx_ref[...]
    gate_all[0] = gate_ref[...]
    for kb in range(n_kb):
        xall[0, kb] = x_ref[:, kb * kb_w:(kb + 1) * kb_w]

    rows_s = round_up(n_slot, 8)
    sub = lax.broadcasted_iota(jnp.int32, (rows_s, n_slot), 0)
    lane = lax.broadcasted_iota(jnp.int32, (rows_s, n_slot), 1)
    my_row = tab_ref[pl.ds(me, 1), :].astype(F32)
    e_col = jnp.sum(jnp.where(sub == lane, my_row, 0.0), axis=1, keepdims=True)
    e_col = jnp.where(sub[:, 0:1] < n_slot, e_col, -2.0)
    total = jnp.zeros((rows_s, n_slot), F32)
    before = jnp.zeros((rows_s, n_slot), F32)
    for d in range(n_dev):
        same = jnp.where(tab_ref[d:d + 1, :].astype(F32) == e_col, 1.0, 0.0)
        total = total + same
        before = before + same * jnp.where(d < me, 1.0, 0.0)
    copies = jnp.sum(total, axis=1, keepdims=True)
    my_rank = jnp.sum(before, axis=1, keepdims=True)
    r = lax.broadcasted_iota(jnp.int32, (cap, LANES), 0)
    for s in range(n_slot):
        want = r.astype(F32) * copies[s:s + 1, :] + my_rank[s:s + 1, :]
        trk[s * cap:(s + 1) * cap, :] = jnp.where(r < bound, want, -2.0)

    def clear(q, carry):
        acc[q] = jnp.zeros(acc.shape[1:], F32)
        return carry

    lax.fori_loop(0, acc.shape[0], clear, 0)
    stage_near(0)
    start_near(AHEAD)

    for m in metas:
        m.wait_recv()
    lane_tok = n_tok
    earlier = (lax.broadcasted_iota(jnp.int32, (lane_tok, lane_tok), 0)
               < lax.broadcasted_iota(jnp.int32, (lane_tok, lane_tok), 1)).astype(F32).astype(BF16)
    rows_src = n_slot * cap
    rows_pad = round_up(rows_src, LANES)

    def route(j, carry):
        idx = idx_all[j].astype(F32)
        gates = gate_all[j]
        has = jnp.zeros((rows_s, lane_tok), F32)
        gate = jnp.zeros((rows_s, lane_tok), F32)
        for q in range(n_top):
            hit = idx[q:q + 1, :] == e_col
            has = jnp.where(hit, 1.0, has)
            gate = jnp.where(hit, gates[q:q + 1, :], gate)
        rank = jnp.where(has > 0.0, dot(has.astype(BF16), earlier), -1.0)
        parts = []
        for s in range(n_slot):
            hit = rank[s:s + 1, :] == trk[s * cap:(s + 1) * cap, 0:1]
            g_buf[j, s * cap:(s + 1) * cap, :] = jnp.where(hit, 1.0, 0.0).astype(BF16)
            parts.append(jnp.where(hit, gate[s:s + 1, :], 0.0))
        if rows_pad > rows_src:
            parts.append(jnp.zeros((rows_pad - rows_src, lane_tok), F32))
        left_over = jnp.transpose(jnp.concatenate(parts, axis=0))[:, :rows_src]
        for n in range(3):
            term = left_over.astype(BF16)
            c_buf[j, n * n_tok:(n + 1) * n_tok, :] = term
            left_over = left_over - term.astype(F32)
        return carry

    lax.fori_loop(0, n_dev, route, 0)
    stage_near(1)
    start_near(AHEAD + 1)
    stage_far(0)

    chunks = [(n, min(2 * LANES, d_ff - n)) for n in range(0, d_ff, 2 * LANES)]
    n_mid = d_ff // LANES
    groups = [range(s, min(s + GROUP, n_slot)) for s in range(0, n_slot, GROUP)]

    def up_block(kb, last, after):
        for off in range(CHIPS):
            across(kb, off).wait_recv()

        def gather(j, carry):
            rows = dot(g_buf[j], xall[j, kb]).astype(BF16)
            for s in range(n_slot):
                xg[s, pl.ds(pl.multiple_of(j * cap, cap), cap), :] = rows[s * cap:(s + 1) * cap]
            return carry

        lax.fori_loop(0, n_dev, gather, 0)
        for g, group in enumerate(groups):
            for s in group:
                up_load(kb, s).wait()
            for s in group:
                for n0, nw in chunks:
                    v = dot(xg[s], wu[s, :, n0:n0 + nw])
                    for n in range(0, nw, LANES):
                        q = s * n_mid + (n0 + n) // LANES
                        part = acc[q, :d_mid, :] + v[:, n:n + LANES]
                        if last:
                            h_buf[s, :, n0 + n:n0 + n + LANES] = gelu(part).astype(BF16)
                        else:
                            acc[q, :d_mid, :] = part
            if not last:
                for s in group:
                    up_load(kb + 1, s).start()
            if g in after:
                after[g]()

    def up_step(kb, carry):
        def near_2():
            @pl.when(kb + 2 < n_kb)
            def _():
                stage_near(kb + 2)

            @pl.when(kb + 2 + AHEAD < n_kb)
            def _():
                start_near(kb + 2 + AHEAD)

        up_block(kb, False, {0: near_2, 1: lambda: stage_far(kb + 1)})
        return carry

    lax.fori_loop(0, n_kb - 1, up_step, 0)
    up_block(n_kb - 1, True, {})

    def mine(cb, off, h):
        return (cb * CHIPS + off) * 2 + h

    def staged(cb, off, h):
        return n_cb * CHIPS * 2 + ((cb % STAGES) * CHIPS + off) * 2 + h

    tok = pl.ds(0, n_tok)
    to_sib = [[rcopy(acc.at[pl.ds(staged(cb, off, 0), 2), tok], sib_in.at[cb, off], ps_ss.at[cb, off], ps_rs.at[cb, off], sib)
               for off in range(CHIPS)] for cb in range(n_cb)]
    to_far = [(rcopy(acc.at[mine(cb, 2, 0), tok], far_in.at[cb, 0], pf_ss.at[cb, 0], pf_rs.at[cb, 0], right),
               rcopy(acc.at[mine(cb, 2, 1), tok], far_in.at[cb, 1], pf_ss.at[cb, 1], pf_rs.at[cb, 1], left)) for cb in range(n_cb)]
    to_dir = [(rcopy(acc.at[mine(cb, 1, 1), tok], dir_in.at[cb, 0], pd_ss.at[cb, 0], pd_rs.at[cb, 0], right),
               rcopy(acc.at[mine(cb, 3, 0), tok], dir_in.at[cb, 1], pd_ss.at[cb, 1], pd_rs.at[cb, 1], left)) for cb in range(n_cb)]
    to_mrg = [(rcopy(far_in.at[cb, 0], mrg_in.at[cb, 0], pm_ss.at[cb, 0], pm_rs.at[cb, 0], right),
               rcopy(far_in.at[cb, 1], mrg_in.at[cb, 1], pm_ss.at[cb, 1], pm_rs.at[cb, 1], left)) for cb in range(n_cb)]

    def merge(cb):
        to_far[cb][0].wait_recv()
        far_in[cb, 0] = far_in[cb, 0] + acc[mine(cb, 1, 0), :n_tok, :]
        to_mrg[cb][0].start()
        to_far[cb][1].wait_recv()
        far_in[cb, 1] = far_in[cb, 1] + acc[mine(cb, 3, 1), :n_tok, :]
        to_mrg[cb][1].start()

    def finish(cb):
        for h in range(2):
            to_mrg[cb][h].wait_recv()
            to_dir[cb][1 - h].wait_recv()
            out = acc[mine(cb, 0, h), :n_tok, :] + mrg_in[cb, h] + dir_in[cb, 1 - h]
            y_ref[:, cb * cb_w + h * LANES:cb * cb_w + (h + 1) * LANES] = out.astype(BF16)

    for cb in range(n_cb):
        def down(s, carry, cb=cb):
            down_load(cb, s).wait()
            out = dot(h_buf[s], wd[s]).astype(BF16)
            for j in range(n_dev):
                o_buf[j, pl.ds(pl.multiple_of(s * cap, cap), cap), :] = out[j * cap:(j + 1) * cap]
            if cb + 1 < n_cb:
                down_load(cb + 1, s).start()
            return carry

        lax.fori_loop(0, n_slot, down, 0)
        if cb >= STAGES:
            for off in range(CHIPS):
                to_sib[cb - STAGES][off].wait_send()

        def combine(off, carry, dc, first):
            v = dot(c_buf[2 * off + dc], o_buf[2 * off + dc])
            v = (v[2 * n_tok:] + v[n_tok:2 * n_tok]) + v[:n_tok]
            acc[first + 2 * off, :n_tok, :] = v[:, :LANES]
            acc[first + 2 * off + 1, :n_tok, :] = v[:, LANES:]
            return carry

        lax.fori_loop(0, CHIPS, functools.partial(combine, dc=1, first=staged(cb, 0, 0)), 0)
        for off in (2, 1, 3, 0):
            to_sib[cb][off].start()
        lax.fori_loop(0, CHIPS, functools.partial(combine, dc=0, first=mine(cb, 0, 0)), 0)
        if cb >= LAG:
            finish(cb - LAG)
        for off in (2, 1, 3, 0):
            to_sib[cb][off].wait_recv()
            for h in range(2):
                q = mine(cb, off, h)
                acc[q, :n_tok, :] = acc[q, :n_tok, :] + sib_in[cb, off, h]
            if off == 2:
                to_far[cb][0].start()
                to_far[cb][1].start()
            elif off:
                to_dir[cb][0 if off == 1 else 1].start()
        if cb >= 1:
            merge(cb - 1)
    merge(n_cb - 1)
    for cb in range(max(0, n_cb - LAG), n_cb):
        finish(cb)

    for m in metas:
        m.wait_send()

    def drain(kb, carry):
        for c in near(kb) + relay(kb) + tuple(across(kb, off) for off in range(CHIPS)):
            c.wait_send()
        return carry

    lax.fori_loop(0, n_kb, drain, 0)
    for cb in range(n_cb):
        for c in to_far[cb] + to_dir[cb] + to_mrg[cb]:
            c.wait_send()
        if cb + STAGES >= n_cb:
            for c in to_sib[cb]:
                c.wait_send()


def solution(mesh):
    assert mesh.shape["ep"] == 2 * CHIPS

    def group_layer(tokens, topk_idx, topk_w, w_up, w_down, slot_expert):
        n_tok, d_model = tokens.shape
        n_top = topk_idx.shape[1]
        n_dev, n_slot = slot_expert.shape
        d_ff = w_up.shape[-1]
        bound = slot_bound(n_tok, n_top, n_dev, n_slot)
        cap = round_up(bound, 16)
        kb_w, cb_w = 2 * LANES, 2 * LANES
        n_kb, n_cb = d_model // kb_w, d_model // cb_w
        d_mid = n_dev * cap
        rows_src = n_slot * cap
        n_acc = max(n_slot * (d_ff // LANES), (n_cb + STAGES) * CHIPS * 2)
        cfg = dict(bound=bound, cap=cap, kb_w=kb_w, cb_w=cb_w)
        dma = pltpu.SemaphoreType.DMA
        vmem = pl.BlockSpec(memory_space=pltpu.VMEM)
        hbm = pl.BlockSpec(memory_space=pl.ANY)
        return pl.pallas_call(
            functools.partial(moe_kernel, cfg),
            out_shape=jax.ShapeDtypeStruct((n_tok, d_model), BF16),
            in_specs=[vmem, vmem, vmem, vmem, hbm, hbm],
            out_specs=vmem,
            scratch_shapes=[
                pltpu.VMEM((n_dev, n_kb, n_tok, kb_w), BF16),
                pltpu.VMEM((n_dev, n_top, n_tok), jnp.int32),
                pltpu.VMEM((n_dev, n_top, n_tok), F32),
                pltpu.VMEM((rows_src, LANES), F32),
                pltpu.VMEM((n_dev, rows_src, n_tok), BF16),
                pltpu.VMEM((n_dev, 3 * n_tok, rows_src), BF16),
                pltpu.VMEM((n_slot, d_mid, kb_w), BF16),
                pltpu.VMEM((n_acc, max(d_mid, n_tok), LANES), F32),
                pltpu.VMEM((n_slot, d_mid, d_ff), BF16),
                pltpu.VMEM((n_dev, rows_src, cb_w), BF16),
                pltpu.VMEM((n_slot, kb_w, d_ff), BF16),
                pltpu.VMEM((n_slot, d_ff, cb_w), BF16),
                pltpu.VMEM((n_cb, CHIPS, 2, n_tok, LANES), F32),
                pltpu.VMEM((n_cb, 2, n_tok, LANES), F32),
                pltpu.VMEM((n_cb, 2, n_tok, LANES), F32),
                pltpu.VMEM((n_cb, 2, n_tok, LANES), F32),
                dma((n_dev - 1, 2)), dma((n_dev - 1, 2)),
                dma((n_kb, 2)), dma((n_kb, 2)), dma((n_kb, 2)), dma((n_kb, 2)),
                dma((n_kb, CHIPS)), dma((n_kb, CHIPS)),
                dma((n_slot,)), dma((n_slot,)),
                dma((n_cb, CHIPS)), dma((n_cb, CHIPS)),
                dma((n_cb, 2)), dma((n_cb, 2)), dma((n_cb, 2)), dma((n_cb, 2)), dma((n_cb, 2)), dma((n_cb, 2)),
            ],
            compiler_params=pltpu.CompilerParams(collective_id=0, has_side_effects=True, vmem_limit_bytes=67_000_000),
        )(tokens, topk_idx.T, topk_w.T, slot_expert, w_up, w_down)

    row_spec = P(('dp', 'ep'), None)
    weight_spec = P('ep', None, None, None)
    return jax.shard_map(group_layer, mesh=mesh, in_specs=(row_spec, row_spec, row_spec, weight_spec, weight_spec, P(None, None)),
                         out_specs=row_spec, check_vma=False)
```

time: 147 us -> 122 us (0.83)
  Pallas kernels: 140 us -> 120 us
  local copies, waits for them, and re-layouts: 4.52 us -> 2.09 us
  other arithmetic: 2.34 us -> 0 us
    pallas_call x1, Pallas kernels: 140 us -> 120 us  [group_layer(): pl.pallas_call(functools.partial(moe_kernel, cfg), out_shape=jax.ShapeDty...]
where the time goes in v2:
time: 122 us
  Pallas kernels  120 us (98%)
  local copies, waits for them, and re-layouts  2.09 us (2%)
    pallas_call x1, Pallas kernels, group_layer(): pl.pallas_call(functools.partial(moe_kernel, cfg), out_shape=jax.ShapeDty...  120 us

profile of v2, /device:TPU:81, one launch (start us, length us, event | category | flops | bytes accessed | tf_op | source)
XLA Modules:
  0.0 122.2 jit_solution(9615522318744235525)
XLA Ops:
  0.0 120.1 %shard_map.64 = bf16[192,2048]{1,0:T(8,128)(2,1)} custom-call(bf16[192,2048]{1,0:T(8,128)(2,1)} %x_ref.1, s32[6,192]{1,0:T(8,128)} %bitcast.2, f32[6,192]{1,0:T(8,128)} %bitcast.3, s32[8,9]{1,0:T(8,128)} %tab_ref.1, bf16[1,9,2048,1408]{3,2,1,0:T(8,128)(2,1)} %wup_ref.1, bf16[1,9,1408,2048]{3,2,1,0:T(8,128)(2,1)} %wdn_ref.1), custom_call_target="tpu_custom_call" | custom-call | tf_op jit(solution)/shard_map/pallas_call | solution.py:352
  120.1 2.1 %copy.8 = bf16[192,2048]{1,0:T(8,128)(2,1)} copy(bf16[192,2048]{1,0:T(8,128)(2,1)} %shard_map.64) | data formatting | bytes 1572864

commit v3 on v2

--- a/solution.py
+++ b/solution.py
@@ -62,7 +62,7 @@
         return pltpu.make_async_copy(wup_ref.at[0, s, pl.ds(pl.multiple_of(kb * kb_w, kb_w), kb_w), :], wu.at[s], wu_s.at[s])
 
     def down_load(cb, s):
-        return pltpu.make_async_copy(wdn_ref.at[0, s, :, pl.ds(cb * cb_w, cb_w)], wd.at[s], wd_s.at[s])
+        return pltpu.make_async_copy(wdn_ref.at[0, s, :, pl.ds(pl.multiple_of(cb * cb_w, cb_w), cb_w)], wd.at[s], wd_s.at[s])
 
     barrier = pltpu.get_barrier_semaphore()
     peers = [(dx, dc) for dx in range(CHIPS) for dc in range(2) if dx or dc]
@@ -196,13 +196,10 @@
         for off in range(CHIPS):
             across(kb, off).wait_recv()
 
-        def gather(j, carry):
+        for j in range(n_dev):
             rows = dot(g_buf[j], xall[j, kb]).astype(BF16)
             for s in range(n_slot):
-                xg[s, pl.ds(pl.multiple_of(j * cap, cap), cap), :] = rows[s * cap:(s + 1) * cap]
-            return carry
-
-        lax.fori_loop(0, n_dev, gather, 0)
+                xg[s, j * cap:(j + 1) * cap, :] = rows[s * cap:(s + 1) * cap]
         for g, group in enumerate(groups):
             for s in group:
                 up_load(kb, s).wait()
@@ -245,70 +242,88 @@
         return n_cb * CHIPS * 2 + ((cb % STAGES) * CHIPS + off) * 2 + h
 
     tok = pl.ds(0, n_tok)
-    to_sib = [[rcopy(acc.at[pl.ds(staged(cb, off, 0), 2), tok], sib_in.at[cb, off], ps_ss.at[cb, off], ps_rs.at[cb, off], sib)
-               for off in range(CHIPS)] for cb in range(n_cb)]
-    to_far = [(rcopy(acc.at[mine(cb, 2, 0), tok], far_in.at[cb, 0], pf_ss.at[cb, 0], pf_rs.at[cb, 0], right),
-               rcopy(acc.at[mine(cb, 2, 1), tok], far_in.at[cb, 1], pf_ss.at[cb, 1], pf_rs.at[cb, 1], left)) for cb in range(n_cb)]
-    to_dir = [(rcopy(acc.at[mine(cb, 1, 1), tok], dir_in.at[cb, 0], pd_ss.at[cb, 0], pd_rs.at[cb, 0], right),
-               rcopy(acc.at[mine(cb, 3, 0), tok], dir_in.at[cb, 1], pd_ss.at[cb, 1], pd_rs.at[cb, 1], left)) for cb in range(n_cb)]
-    to_mrg = [(rcopy(far_in.at[cb, 0], mrg_in.at[cb, 0], pm_ss.at[cb, 0], pm_rs.at[cb, 0], right),
-               rcopy(far_in.at[cb, 1], mrg_in.at[cb, 1], pm_ss.at[cb, 1], pm_rs.at[cb, 1], left)) for cb in range(n_cb)]
+
+    def to_sib(cb, off):
+        return rcopy(acc.at[pl.ds(staged(cb, off, 0), 2), tok], sib_in.at[cb, off], ps_ss.at[cb, off], ps_rs.at[cb, off], sib)
+
+    def to_far(cb):
+        return (rcopy(acc.at[mine(cb, 2, 0), tok], far_in.at[cb, 0], pf_ss.at[cb, 0], pf_rs.at[cb, 0], right),
+                rcopy(acc.at[mine(cb, 2, 1), tok], far_in.at[cb, 1], pf_ss.at[cb, 1], pf_rs.at[cb, 1], left))
+
+    def to_dir(cb):
+        return (rcopy(acc.at[mine(cb, 1, 1), tok], dir_in.at[cb, 0], pd_ss.at[cb, 0], pd_rs.at[cb, 0], right),
+                rcopy(acc.at[mine(cb, 3, 0), tok], dir_in.at[cb, 1], pd_ss.at[cb, 1], pd_rs.at[cb, 1], left))
+
+    def to_mrg(cb):
+        return (rcopy(far_in.at[cb, 0], mrg_in.at[cb, 0], pm_ss.at[cb, 0], pm_rs.at[cb, 0], right),
+                rcopy(far_in.at[cb, 1], mrg_in.at[cb, 1], pm_ss.at[cb, 1], pm_rs.at[cb, 1], left))
 
     def merge(cb):
-        to_far[cb][0].wait_recv()
-        far_in[cb, 0] = far_in[cb, 0] + acc[mine(cb, 1, 0), :n_tok, :]
-        to_mrg[cb][0].start()
-        to_far[cb][1].wait_recv()
-        far_in[cb, 1] = far_in[cb, 1] + acc[mine(cb, 3, 1), :n_tok, :]
-        to_mrg[cb][1].start()
+        for h, off in ((0, 1), (1, prev)):
+            to_far(cb)[h].wait_recv()
+            far_in[cb, h] = far_in[cb, h] + acc[mine(cb, off, h), :n_tok, :]
+            to_mrg(cb)[h].start()
 
     def finish(cb):
         for h in range(2):
-            to_mrg[cb][h].wait_recv()
-            to_dir[cb][1 - h].wait_recv()
+            to_mrg(cb)[h].wait_recv()
+            to_dir(cb)[1 - h].wait_recv()
             out = acc[mine(cb, 0, h), :n_tok, :] + mrg_in[cb, h] + dir_in[cb, 1 - h]
-            y_ref[:, cb * cb_w + h * LANES:cb * cb_w + (h + 1) * LANES] = out.astype(BF16)
-
-    for cb in range(n_cb):
-        def down(s, carry, cb=cb):
-            down_load(cb, s).wait()
-            out = dot(h_buf[s], wd[s]).astype(BF16)
-            for j in range(n_dev):
-                o_buf[j, pl.ds(pl.multiple_of(s * cap, cap), cap), :] = out[j * cap:(j + 1) * cap]
-            if cb + 1 < n_cb:
-                down_load(cb + 1, s).start()
-            return carry
-
-        lax.fori_loop(0, n_slot, down, 0)
-        if cb >= STAGES:
+            y_ref[:, pl.ds(pl.multiple_of(cb * cb_w + h * LANES, LANES), LANES)] = out.astype(BF16)
+
+    def combine(j, q):
+        v = dot(c_buf[j], o_buf[j])
+        v = (v[2 * n_tok:] + v[n_tok:2 * n_tok]) + v[:n_tok]
+        for h in range(2):
+            acc[q + h, :n_tok, :] = v[:, h * LANES:(h + 1) * LANES]
+
+    def down_step(cb, carry):
+        for group in groups:
+            for s in group:
+                down_load(cb, s).wait()
+            for s in group:
+                out = dot(h_buf[s], wd[s]).astype(BF16)
+                for j in range(n_dev):
+                    o_buf[j, s * cap:(s + 1) * cap, :] = out[j * cap:(j + 1) * cap]
+
+            @pl.when(cb + 1 < n_cb)
+            def _():
+                for s in group:
+                    down_load(cb + 1, s).start()
+
+        @pl.when(cb >= STAGES)
+        def _():
             for off in range(CHIPS):
-                to_sib[cb - STAGES][off].wait_send()
-
-        def combine(off, carry, dc, first):
-            v = dot(c_buf[2 * off + dc], o_buf[2 * off + dc])
-            v = (v[2 * n_tok:] + v[n_tok:2 * n_tok]) + v[:n_tok]
-            acc[first + 2 * off, :n_tok, :] = v[:, :LANES]
-            acc[first + 2 * off + 1, :n_tok, :] = v[:, LANES:]
-            return carry
-
-        lax.fori_loop(0, CHIPS, functools.partial(combine, dc=1, first=staged(cb, 0, 0)), 0)
-        for off in (2, 1, 3, 0):
-            to_sib[cb][off].start()
-        lax.fori_loop(0, CHIPS, functools.partial(combine, dc=0, first=mine(cb, 0, 0)), 0)
-        if cb >= LAG:
+                to_sib(cb - STAGES, off).wait_send()
+
+        order = (2, 1, prev, 0)
+        for off in order:
+            combine(2 * off + 1, staged(cb, off, 0))
+            to_sib(cb, off).start()
+        for off in order:
+            combine(2 * off, mine(cb, off, 0))
+
+        @pl.when(cb >= LAG)
+        def _():
             finish(cb - LAG)
-        for off in (2, 1, 3, 0):
-            to_sib[cb][off].wait_recv()
+
+        for off in order:
+            to_sib(cb, off).wait_recv()
             for h in range(2):
                 q = mine(cb, off, h)
                 acc[q, :n_tok, :] = acc[q, :n_tok, :] + sib_in[cb, off, h]
             if off == 2:
-                to_far[cb][0].start()
-                to_far[cb][1].start()
+                for c in to_far(cb):
+                    c.start()
             elif off:
-                to_dir[cb][0 if off == 1 else 1].start()
-        if cb >= 1:
+                to_dir(cb)[0 if off == 1 else 1].start()
+
+        @pl.when(cb >= 1)
+        def _():
             merge(cb - 1)
+        return carry
+
+    lax.fori_loop(0, n_cb, down_step, 0)
     merge(n_cb - 1)
     for cb in range(max(0, n_cb - LAG), n_cb):
         finish(cb)
@@ -322,12 +337,16 @@
         return carry
 
     lax.fori_loop(0, n_kb, drain, 0)
-    for cb in range(n_cb):
-        for c in to_far[cb] + to_dir[cb] + to_mrg[cb]:
+
+    def drain_sums(cb, carry):
+        for c in to_far(cb) + to_dir(cb) + to_mrg(cb):
             c.wait_send()
-        if cb + STAGES >= n_cb:
-            for c in to_sib[cb]:
-                c.wait_send()
+        return carry
+
+    lax.fori_loop(0, n_cb, drain_sums, 0)
+    for cb in range(max(0, n_cb - STAGES), n_cb):
+        for off in range(CHIPS):
+            to_sib(cb, off).wait_send()
 
 
 def solution(mesh):

time: 122 us -> 111 us (0.910)
  Pallas kernels: 120 us -> 108 us
    pallas_call x1, Pallas kernels: 120 us -> 108 us  [group_layer(): pl.pallas_call(functools.partial(moe_kernel, cfg), out_shape=jax.ShapeDty...]
where the time goes in v3:
time: 111 us; the launch traced here: 110 us
  Pallas kernels  108 us (97%)
  local copies, waits for them, and re-layouts  2.09 us (2%)
    pallas_call x1, Pallas kernels, group_layer(): pl.pallas_call(functools.partial(moe_kernel, cfg), out_shape=jax.ShapeDty...  108 us

profile of v3, /device:TPU:81, one launch (start us, length us, event | category | flops | bytes accessed | tf_op | source)
XLA Modules:
  0.0 110.5 jit_solution(8617102695445305443)
XLA Ops:
  0.0 108.4 %shard_map.64 = bf16[192,2048]{1,0:T(8,128)(2,1)} custom-call(bf16[192,2048]{1,0:T(8,128)(2,1)} %x_ref.1, s32[6,192]{1,0:T(8,128)} %bitcast.2, f32[6,192]{1,0:T(8,128)} %bitcast.3, s32[8,9]{1,0:T(8,128)} %tab_ref.1, bf16[1,9,2048,1408]{3,2,1,0:T(8,128)(2,1)} %wup_ref.1, bf16[1,9,1408,2048]{3,2,1,0:T(8,128)(2,1)} %wdn_ref.1), custom_call_target="tpu_custom_call" | custom-call | tf_op jit(solution)/shard_map/pallas_call | solution.py:371
  108.4 2.1 %copy.8 = bf16[192,2048]{1,0:T(8,128)(2,1)} copy(bf16[192,2048]{1,0:T(8,128)(2,1)} %shard_map.64) | data formatting | bytes 1572864

commit v4 on v3

--- a/solution.py
+++ b/solution.py
@@ -36,15 +36,18 @@
 
 
 def moe_kernel(cfg, x_ref, idx_ref, gate_ref, tab_ref, wup_ref, wdn_ref, y_ref,
-               xall, idx_all, gate_all, trk, g_buf, c_buf, xg, acc, h_buf, o_buf, wu, wd, sib_in, far_in, dir_in, mrg_in,
+               xall, idx_all, gate_all, trk, g_buf, c_buf, xg, xg_odd, acc, h_buf, o_buf, o_odd, wu, wd, sib_in, far_in, dir_in, mrg_in,
                meta_ss, meta_rs, near_ss, near_rs, rel_ss, rel_rs, sib_ss, sib_rs, wu_s, wd_s,
                ps_ss, ps_rs, pf_ss, pf_rs, pd_ss, pd_rs, pm_ss, pm_rs):
     bound, cap, kb_w, cb_w = (cfg[k] for k in ("bound", "cap", "kb_w", "cb_w"))
+    odd = bound - cap
     n_tok, d_model = x_ref.shape
     n_top = idx_ref.shape[0]
     n_dev, n_slot = tab_ref.shape
     d_ff = wup_ref.shape[-1]
-    d_mid = n_dev * cap
+    d_main, d_mid = n_dev * cap, n_dev * bound
+    rows_s = round_up(n_slot, 16)
+    rows_main, rows_src = n_slot * cap, n_slot * cap + odd * rows_s
     n_kb, n_cb = d_model // kb_w, d_model // cb_w
     half = n_tok // 2
     me = lax.axis_index("ep")
@@ -124,7 +127,6 @@
     for kb in range(n_kb):
         xall[0, kb] = x_ref[:, kb * kb_w:(kb + 1) * kb_w]
 
-    rows_s = round_up(n_slot, 8)
     sub = lax.broadcasted_iota(jnp.int32, (rows_s, n_slot), 0)
     lane = lax.broadcasted_iota(jnp.int32, (rows_s, n_slot), 1)
     my_row = tab_ref[pl.ds(me, 1), :].astype(F32)
@@ -141,7 +143,8 @@
     r = lax.broadcasted_iota(jnp.int32, (cap, LANES), 0)
     for s in range(n_slot):
         want = r.astype(F32) * copies[s:s + 1, :] + my_rank[s:s + 1, :]
-        trk[s * cap:(s + 1) * cap, :] = jnp.where(r < bound, want, -2.0)
+        trk[s * cap:(s + 1) * cap, :] = want
+    o_odd[...] = jnp.zeros_like(o_odd)
 
     def clear(q, carry):
         acc[q] = jnp.zeros(acc.shape[1:], F32)
@@ -156,7 +159,6 @@
     lane_tok = n_tok
     earlier = (lax.broadcasted_iota(jnp.int32, (lane_tok, lane_tok), 0)
                < lax.broadcasted_iota(jnp.int32, (lane_tok, lane_tok), 1)).astype(F32).astype(BF16)
-    rows_src = n_slot * cap
     rows_pad = round_up(rows_src, LANES)
 
     def route(j, carry):
@@ -174,6 +176,11 @@
             hit = rank[s:s + 1, :] == trk[s * cap:(s + 1) * cap, 0:1]
             g_buf[j, s * cap:(s + 1) * cap, :] = jnp.where(hit, 1.0, 0.0).astype(BF16)
             parts.append(jnp.where(hit, gate[s:s + 1, :], 0.0))
+        for n in range(odd):
+            hit = rank == float(cap + n) * copies + my_rank
+            first = rows_main + n * rows_s
+            g_buf[j, first:first + rows_s, :] = jnp.where(hit, 1.0, 0.0).astype(BF16)
+            parts.append(jnp.where(hit, gate, 0.0))
         if rows_pad > rows_src:
             parts.append(jnp.zeros((rows_pad - rows_src, lane_tok), F32))
         left_over = jnp.transpose(jnp.concatenate(parts, axis=0))[:, :rows_src]
@@ -197,9 +204,19 @@
             across(kb, off).wait_recv()
 
         for j in range(n_dev):
-            rows = dot(g_buf[j], xall[j, kb]).astype(BF16)
+            rows = dot(g_buf[j], xall[j, kb])
+            main = rows[:rows_main].astype(BF16)
             for s in range(n_slot):
-                xg[s, j * cap:(j + 1) * cap, :] = rows[s * cap:(s + 1) * cap]
+                xg[s, j * cap:(j + 1) * cap, :] = main[s * cap:(s + 1) * cap]
+            for n in range(odd):
+                first = rows_main + n * rows_s
+                for h in range(kb_w // LANES):
+                    xg_odd[n, h, pl.ds(j, rows_s, stride=n_dev), :] = rows[first:first + rows_s, h * LANES:(h + 1) * LANES]
+        for n in range(odd):
+            for h in range(kb_w // LANES):
+                for s in range(n_slot):
+                    xg[s, d_main + n * n_dev:d_main + (n + 1) * n_dev, h * LANES:(h + 1) * LANES] = (
+                        xg_odd[n, h, s * n_dev:(s + 1) * n_dev, :].astype(BF16))
         for g, group in enumerate(groups):
             for s in group:
                 up_load(kb, s).wait()
@@ -282,14 +299,25 @@
             for s in group:
                 down_load(cb, s).wait()
             for s in group:
-                out = dot(h_buf[s], wd[s]).astype(BF16)
+                out = dot(h_buf[s], wd[s])
+                main = out[:d_main].astype(BF16)
                 for j in range(n_dev):
-                    o_buf[j, s * cap:(s + 1) * cap, :] = out[j * cap:(j + 1) * cap]
+                    o_buf[j, s * cap:(s + 1) * cap, :] = main[j * cap:(j + 1) * cap]
+                for n in range(odd):
+                    first = d_main + n * n_dev
+                    for h in range(cb_w // LANES):
+                        o_odd[n, h, pl.ds(s, n_dev, stride=rows_s), :] = out[first:first + n_dev, h * LANES:(h + 1) * LANES]
 
             @pl.when(cb + 1 < n_cb)
             def _():
                 for s in group:
                     down_load(cb + 1, s).start()
+
+        for n in range(odd):
+            first = rows_main + n * rows_s
+            for h in range(cb_w // LANES):
+                for j in range(n_dev):
+                    o_buf[j, first:first + rows_s, h * LANES:(h + 1) * LANES] = o_odd[n, h, j * rows_s:(j + 1) * rows_s, :].astype(BF16)
 
         @pl.when(cb >= STAGES)
         def _():
@@ -358,11 +386,12 @@
         n_dev, n_slot = slot_expert.shape
         d_ff = w_up.shape[-1]
         bound = slot_bound(n_tok, n_top, n_dev, n_slot)
-        cap = round_up(bound, 16)
+        cap = bound // 8 * 8
+        odd, rows_s = bound - cap, round_up(n_slot, 16)
         kb_w, cb_w = 2 * LANES, 2 * LANES
         n_kb, n_cb = d_model // kb_w, d_model // cb_w
-        d_mid = n_dev * cap
-        rows_src = n_slot * cap
+        d_mid = n_dev * bound
+        rows_src = n_slot * cap + odd * rows_s
         n_acc = max(n_slot * (d_ff // LANES), (n_cb + STAGES) * CHIPS * 2)
         cfg = dict(bound=bound, cap=cap, kb_w=kb_w, cb_w=cb_w)
         dma = pltpu.SemaphoreType.DMA
@@ -377,13 +406,15 @@
                 pltpu.VMEM((n_dev, n_kb, n_tok, kb_w), BF16),
                 pltpu.VMEM((n_dev, n_top, n_tok), jnp.int32),
                 pltpu.VMEM((n_dev, n_top, n_tok), F32),
-                pltpu.VMEM((rows_src, LANES), F32),
+                pltpu.VMEM((n_slot * cap, LANES), F32),
                 pltpu.VMEM((n_dev, rows_src, n_tok), BF16),
                 pltpu.VMEM((n_dev, 3 * n_tok, rows_src), BF16),
                 pltpu.VMEM((n_slot, d_mid, kb_w), BF16),
+                pltpu.VMEM((odd, kb_w // LANES, rows_s * n_dev, LANES), F32),
                 pltpu.VMEM((n_acc, max(d_mid, n_tok), LANES), F32),
                 pltpu.VMEM((n_slot, d_mid, d_ff), BF16),
                 pltpu.VMEM((n_dev, rows_src, cb_w), BF16),
+                pltpu.VMEM((odd, cb_w // LANES, n_dev * rows_s, LANES), F32),
                 pltpu.VMEM((n_slot, kb_w, d_ff), BF16),
                 pltpu.VMEM((n_slot, d_ff, cb_w), BF16),
                 pltpu.VMEM((n_cb, CHIPS, 2, n_tok, LANES), F32),

time: 111 us -> 107 us (0.964)
  Pallas kernels: 108 us -> 104 us
    pallas_call x1, Pallas kernels: 108 us -> 104 us  [group_layer(): pl.pallas_call(functools.partial(moe_kernel, cfg), out_shape=jax.ShapeDty...]
where the time goes in v4:
time: 107 us
  Pallas kernels  104 us (97%)
  local copies, waits for them, and re-layouts  2.09 us (2%)
    pallas_call x1, Pallas kernels, group_layer(): pl.pallas_call(functools.partial(moe_kernel, cfg), out_shape=jax.ShapeDty...  104 us

profile of v4, /device:TPU:81, one launch (start us, length us, event | category | flops | bytes accessed | tf_op | source)
XLA Modules:
  0.0 106.6 jit_solution(15554320625862641541)
XLA Ops:
  0.0 104.5 %shard_map.64 = bf16[192,2048]{1,0:T(8,128)(2,1)} custom-call(bf16[192,2048]{1,0:T(8,128)(2,1)} %x_ref.1, s32[6,192]{1,0:T(8,128)} %bitcast.2, f32[6,192]{1,0:T(8,128)} %bitcast.3, s32[8,9]{1,0:T(8,128)} %tab_ref.1, bf16[1,9,2048,1408]{3,2,1,0:T(8,128)(2,1)} %wup_ref.1, bf16[1,9,1408,2048]{3,2,1,0:T(8,128)(2,1)} %wdn_ref.1), custom_call_target="tpu_custom_call" | custom-call | tf_op jit(solution)/shard_map/pallas_call | solution.py:400
  104.5 2.1 %copy.8 = bf16[192,2048]{1,0:T(8,128)(2,1)} copy(bf16[192,2048]{1,0:T(8,128)(2,1)} %shard_map.64) | data formatting | bytes 1572864

commit v5 on v4

v5 whole, which is shorter than its diff:
```python
import functools

import jax
import jax.numpy as jnp
from jax import lax
from jax.experimental import pallas as pl
from jax.experimental.pallas import tpu as pltpu
from jax.sharding import PartitionSpec as P

MESH = pl.DeviceIdType.MESH
F32 = jnp.float32
BF16 = jnp.bfloat16
LANES = 128
CHIPS = 4
AHEAD = 3
STAGES = 4
GROUP = 3
LAG = 3


def slot_bound(n_tok, n_top, n_dev, n_slot):
    base_load = (n_tok * n_top) // (n_dev * n_slot)
    return base_load + base_load // 2 + 1


def round_up(n, m):
    return -(-n // m) * m


def gelu(v):
    return v * (0.5 + 0.5 * jnp.tanh(v * (0.7978845608028654 + (0.7978845608028654 * 0.044715) * (v * v))))


def dot(a, b):
    return lax.dot_general(a, b, (((1,), (0,)), ((), ())), preferred_element_type=F32)


def moe_kernel(cfg, x_ref, idx_ref, gate_ref, tab_ref, wup_ref, wdn_ref, y_ref,
               xall, idx_all, gate_all, tab, trk, g_buf, c_buf, xg, xg_odd, acc, h_buf, o_buf, o_odd, wu, wd, sib_in, far_in, sum_in, y_buf,
               in_s, meta_ss, meta_rs, out_ss, near_rs, rel_rs, sib_rs, wu_s, wd_s, ps_ss, ps_rs, pf_rs, fin_rs, y_s):
    bound, cap, kb_w, cb_w = (cfg[k] for k in ("bound", "cap", "kb_w", "cb_w"))
    odd = bound - cap
    n_tok, d_model = x_ref.shape
    n_top = idx_ref.shape[0]
    n_dev, n_slot = tab_ref.shape
    d_ff = wup_ref.shape[-1]
    d_main, d_mid = n_dev * cap, n_dev * bound
    rows_s = round_up(n_slot, 16)
    rows_main, rows_src = n_slot * cap, n_slot * cap + odd * rows_s
    n_kb, n_cb = d_model // kb_w, d_model // cb_w
    half = n_tok // 2
    me = lax.axis_index("ep")
    chip, core = me // 2, me % 2

    def dev(d_chip, d_core=0):
        return {"ep": ((chip + d_chip) % CHIPS) * 2 + (core + d_core) % 2}

    right, left, sib = dev(1), dev(CHIPS - 1), dev(0, 1)

    def rcopy(src, dst, ss, rs, to):
        return pltpu.make_async_remote_copy(src_ref=src, dst_ref=dst, send_sem=ss, recv_sem=rs, device_id=to, device_id_type=MESH)

    def took(ref, sem):
        rcopy(ref, ref, sem, sem, sib).wait_send()

    def arrived(ref, sem):
        rcopy(ref, ref, sem, sem, sib).wait_recv()

    groups = [(s, min(GROUP, n_slot - s)) for s in range(0, n_slot, GROUP)]

    def up_load(kb, g):
        s, n = groups[g]
        return pltpu.make_async_copy(
            wup_ref.at[0, pl.ds(s, n), pl.ds(pl.multiple_of(kb * kb_w, kb_w), kb_w), :], wu.at[pl.ds(s, n)], wu_s.at[g])

    def down_load(cb, g):
        s, n = groups[g]
        return pltpu.make_async_copy(
            wdn_ref.at[0, pl.ds(s, n), :, pl.ds(pl.multiple_of(cb * cb_w, cb_w), cb_w)], wd.at[pl.ds(s, n)], wd_s.at[g])

    barrier = pltpu.get_barrier_semaphore()
    peers = [(dx, dc) for dx in range(CHIPS) for dc in range(2) if dx or dc]
    for dx, dc in peers:
        pl.semaphore_signal(barrier, inc=1, device_id=dev(dx, dc), device_id_type=MESH)
    in_meta = [pltpu.make_async_copy(idx_ref, idx_all.at[0], in_s.at[1]), pltpu.make_async_copy(gate_ref, gate_all.at[0], in_s.at[2]),
               pltpu.make_async_copy(tab_ref, tab, in_s.at[3])]
    for c in in_meta:
        c.start()
    for kb in range(n_kb):
        pltpu.make_async_copy(x_ref.at[:, pl.ds(kb * kb_w, kb_w)], xall.at[0, kb], in_s.at[0]).start()
    for g in range(len(groups)):
        up_load(0, g).start()
    for c in in_meta:
        c.wait()
    arrived(xall.at[0], in_s.at[0])
    pl.semaphore_wait(barrier, len(peers))

    lo, hi = pl.ds(0, half), pl.ds(half, n_tok - half)
    prev = CHIPS - 1

    def near(kb):
        return (rcopy(xall.at[0, kb], xall.at[2 * prev, kb], out_ss.at[0], near_rs.at[kb], right),
                rcopy(xall.at[0, kb], xall.at[2, kb], out_ss.at[0], near_rs.at[kb], left))

    def relay(kb):
        return (rcopy(xall.at[2 * prev, kb, lo], xall.at[4, kb, lo], out_ss.at[1], rel_rs.at[kb], right),
                rcopy(xall.at[2, kb, hi], xall.at[4, kb, hi], out_ss.at[1], rel_rs.at[kb], left))

    def across(kb, off):
        return rcopy(xall.at[2 * off, kb], xall.at[2 * off + 1, kb], out_ss.at[2], sib_rs.at[kb], sib)

    def start_near(kb):
        for c in near(kb):
            c.start()

    def stage_near(kb):
        arrived(xall.at[pl.ds(0, 2), kb], near_rs.at[kb])
        for c in relay(kb):
            c.start()
        for off in (prev, 1):
            across(kb, off).start()

    def stage_far(kb):
        arrived(xall.at[4, kb], rel_rs.at[kb])
        across(kb, 2).start()

    for dx, dc in peers:
        place = 2 * ((CHIPS - dx) % CHIPS) + dc
        rcopy(idx_all.at[0], idx_all.at[place], meta_ss.at[0], meta_rs.at[0], dev(dx, dc)).start()
        rcopy(gate_all.at[0], gate_all.at[place], meta_ss.at[1], meta_rs.at[1], dev(dx, dc)).start()
    for kb in range(AHEAD):
        start_near(kb)
    for kb in range(n_kb):
        across(kb, 0).start()
    for g in range(len(groups)):
        down_load(0, g).start()

    sub = lax.broadcasted_iota(jnp.int32, (rows_s, n_slot), 0)
    lane = lax.broadcasted_iota(jnp.int32, (rows_s, n_slot), 1)
    my_row = tab[pl.ds(me, 1), :].astype(F32)
    e_col = jnp.sum(jnp.where(sub == lane, my_row, 0.0), axis=1, keepdims=True)
    e_col = jnp.where(sub[:, 0:1] < n_slot, e_col, -2.0)
    total = jnp.zeros((rows_s, n_slot), F32)
    before = jnp.zeros((rows_s, n_slot), F32)
    for d in range(n_dev):
        same = jnp.where(tab[d:d + 1, :].astype(F32) == e_col, 1.0, 0.0)
        total = total + same
        before = before + same * jnp.where(d < me, 1.0, 0.0)
    copies = jnp.sum(total, axis=1, keepdims=True)
    my_rank = jnp.sum(before, axis=1, keepdims=True)
    r = lax.broadcasted_iota(jnp.int32, (cap, LANES), 0)
    for s in range(n_slot):
        want = r.astype(F32) * copies[s:s + 1, :] + my_rank[s:s + 1, :]
        trk[s * cap:(s + 1) * cap, :] = want
    o_odd[...] = jnp.zeros_like(o_odd)

    def clear(q, carry):
        acc[q] = jnp.zeros(acc.shape[1:], F32)
        return carry

    lax.fori_loop(0, acc.shape[0], clear, 0)
    others = pl.ds(1, n_dev - 1)
    arrived(idx_all.at[others], meta_rs.at[0])
    arrived(gate_all.at[others], meta_rs.at[1])
    lane_tok = n_tok
    earlier = (lax.broadcasted_iota(jnp.int32, (lane_tok, lane_tok), 0)
               < lax.broadcasted_iota(jnp.int32, (lane_tok, lane_tok), 1)).astype(F32).astype(BF16)
    rows_pad = round_up(rows_src, LANES)

    def route(j, carry):
        idx = idx_all[j].astype(F32)
        gates = gate_all[j]
        has = jnp.zeros((rows_s, lane_tok), F32)
        gate = jnp.zeros((rows_s, lane_tok), F32)
        for q in range(n_top):
            hit = idx[q:q + 1, :] == e_col
            has = jnp.where(hit, 1.0, has)
            gate = jnp.where(hit, gates[q:q + 1, :], gate)
        rank = jnp.where(has > 0.0, dot(has.astype(BF16), earlier), -1.0)
        parts = []
        for s in range(n_slot):
            hit = rank[s:s + 1, :] == trk[s * cap:(s + 1) * cap, 0:1]
            g_buf[j, s * cap:(s + 1) * cap, :] = jnp.where(hit, 1.0, 0.0).astype(BF16)
            parts.append(jnp.where(hit, gate[s:s + 1, :], 0.0))
        for n in range(odd):
            hit = rank == float(cap + n) * copies + my_rank
            first = rows_main + n * rows_s
            g_buf[j, first:first + rows_s, :] = jnp.where(hit, 1.0, 0.0).astype(BF16)
            parts.append(jnp.where(hit, gate, 0.0))
        if rows_pad > rows_src:
            parts.append(jnp.zeros((rows_pad - rows_src, lane_tok), F32))
        left_over = jnp.transpose(jnp.concatenate(parts, axis=0))[:, :rows_src]
        for n in range(3):
            term = left_over.astype(BF16)
            c_buf[j, n * n_tok:(n + 1) * n_tok, :] = term
            left_over = left_over - term.astype(F32)
        return carry

    lax.fori_loop(0, n_dev, route, 0)
    stage_near(0)
    start_near(AHEAD)
    stage_near(1)
    start_near(AHEAD + 1)
    stage_far(0)

    chunks = [(n, min(2 * LANES, d_ff - n)) for n in range(0, d_ff, 2 * LANES)]
    n_mid = d_ff // LANES

    def up_block(kb, last, after):
        arrived(xall.at[pl.ds(0, CHIPS), kb], sib_rs.at[kb])

        for j in range(n_dev):
            rows = dot(g_buf[j], xall[j, kb])
            main = rows[:rows_main].astype(BF16)
            for s in range(n_slot):
                xg[s, j * cap:(j + 1) * cap, :] = main[s * cap:(s + 1) * cap]
            for n in range(odd):
                first = rows_main + n * rows_s
                for h in range(kb_w // LANES):
                    xg_odd[n, h, pl.ds(j, rows_s, stride=n_dev), :] = rows[first:first + rows_s, h * LANES:(h + 1) * LANES]
        for n in range(odd):
            for h in range(kb_w // LANES):
                for s in range(n_slot):
                    xg[s, d_main + n * n_dev:d_main + (n + 1) * n_dev, h * LANES:(h + 1) * LANES] = (
                        xg_odd[n, h, s * n_dev:(s + 1) * n_dev, :].astype(BF16))
        if last:
            for g in range(len(groups)):
                up_load(kb, g).wait()
        for g, (s0, n_s) in enumerate(groups):
            if not last:
                up_load(kb, g).wait()
            for s in range(s0, s0 + n_s):
                for n0, nw in chunks:
                    v = dot(xg[s], wu[s, :, n0:n0 + nw])
                    for n in range(0, nw, LANES):
                        q = s * n_mid + (n0 + n) // LANES
                        part = acc[q, :d_mid, :] + v[:, n:n + LANES]
                        if last:
                            h_buf[s, :, n0 + n:n0 + n + LANES] = gelu(part).astype(BF16)
                        else:
                            acc[q, :d_mid, :] = part
            if not last:
                up_load(kb + 1, g).start()
            if g in after:
                after[g]()

    def up_step(kb, carry):
        def near_2():
            @pl.when(kb + 2 < n_kb)
            def _():
                stage_near(kb + 2)

            @pl.when(kb + 2 + AHEAD < n_kb)
            def _():
                start_near(kb + 2 + AHEAD)

        up_block(kb, False, {0: near_2, 1: lambda: stage_far(kb + 1)})
        return carry

    lax.fori_loop(0, n_kb - 1, up_step, 0)
    up_block(n_kb - 1, True, {})

    def mine(cb, off, h):
        return (cb * CHIPS + off) * 2 + h

    def staged(cb, off, h):
        return n_cb * CHIPS * 2 + ((cb % STAGES) * CHIPS + off) * 2 + h

    tok = pl.ds(0, n_tok)

    lots = {2: 0, 1: 1, prev: 1, 0: 2}

    def to_sib(cb, off):
        return rcopy(acc.at[pl.ds(staged(cb, off, 0), 2), tok], sib_in.at[cb, off], ps_ss.at[cb % STAGES], ps_rs.at[cb % 2, lots[off]], sib)

    def to_far(cb):
        return (rcopy(acc.at[mine(cb, 2, 0), tok], far_in.at[cb, 0], out_ss.at[3], pf_rs.at[cb], right),
                rcopy(acc.at[mine(cb, 2, 1), tok], far_in.at[cb, 1], out_ss.at[3], pf_rs.at[cb], left))

    def to_dir(cb):
        return (rcopy(acc.at[mine(cb, 1, 1), tok], sum_in.at[cb, 2], out_ss.at[4], fin_rs.at[cb], right),
                rcopy(acc.at[mine(cb, prev, 0), tok], sum_in.at[cb, 3], out_ss.at[4], fin_rs.at[cb], left))

    def to_mrg(cb):
        return (rcopy(far_in.at[cb, 0], sum_in.at[cb, 0], out_ss.at[5], fin_rs.at[cb], right),
                rcopy(far_in.at[cb, 1], sum_in.at[cb, 1], out_ss.at[5], fin_rs.at[cb], left))

    def merge(cb):
        arrived(far_in.at[cb], pf_rs.at[cb])
        for h, off in ((0, 1), (1, prev)):
            far_in[cb, h] = far_in[cb, h] + acc[mine(cb, off, h), :n_tok, :]
            to_mrg(cb)[h].start()

    def y_copy(cb):
        columns = pl.ds(pl.multiple_of(cb * cb_w, cb_w), cb_w)
        return pltpu.make_async_copy(y_buf.at[cb], y_ref.at[:, columns], y_s.at[cb])

    def finish(cb):
        arrived(sum_in.at[cb], fin_rs.at[cb])
        for h in range(2):
            out = acc[mine(cb, 0, h), :n_tok, :] + sum_in[cb, h] + sum_in[cb, 3 - h]
            y_buf[cb, :, h * LANES:(h + 1) * LANES] = out.astype(BF16)
        y_copy(cb).start()

    def add_sib(cb, off):
        for h in range(2):
            q = mine(cb, off, h)
            acc[q, :n_tok, :] = acc[q, :n_tok, :] + sib_in[cb, off, h]

    def combine(j, q):
        v = dot(c_buf[j], o_buf[j])
        v = (v[2 * n_tok:] + v[n_tok:2 * n_tok]) + v[:n_tok]
        for h in range(2):
            acc[q + h, :n_tok, :] = v[:, h * LANES:(h + 1) * LANES]

    def down_step(cb, carry):
        for g, (s0, n_s) in enumerate(groups):
            down_load(cb, g).wait()
            for s in range(s0, s0 + n_s):
                out = dot(h_buf[s], wd[s])
                main = out[:d_main].astype(BF16)
                for j in range(n_dev):
                    o_buf[j, s * cap:(s + 1) * cap, :] = main[j * cap:(j + 1) * cap]
                for n in range(odd):
                    first = d_main + n * n_dev
                    for h in range(cb_w // LANES):
                        o_odd[n, h, pl.ds(s, n_dev, stride=rows_s), :] = out[first:first + n_dev, h * LANES:(h + 1) * LANES]

            @pl.when(cb + 1 < n_cb)
            def _():
                down_load(cb + 1, g).start()

        for n in range(odd):
            first = rows_main + n * rows_s
            for h in range(cb_w // LANES):
                for j in range(n_dev):
                    o_buf[j, first:first + rows_s, h * LANES:(h + 1) * LANES] = o_odd[n, h, j * rows_s:(j + 1) * rows_s, :].astype(BF16)

        @pl.when(cb >= STAGES)
        def _():
            took(acc.at[pl.ds(staged(cb, 0, 0), 2 * CHIPS), tok], ps_ss.at[cb % STAGES])

        def for_sib(off):
            combine(2 * off + 1, staged(cb, off, 0))
            to_sib(cb, off).start()

        for off in (2, 1, prev):
            for_sib(off)
        combine(2 * 2, mine(cb, 2, 0))
        arrived(sib_in.at[cb, 2], ps_rs.at[cb % 2, 0])
        add_sib(cb, 2)
        for c in to_far(cb):
            c.start()
        for_sib(0)
        for off in (1, prev):
            combine(2 * off, mine(cb, off, 0))
        arrived(sib_in.at[cb, pl.ds(0, 2)], ps_rs.at[cb % 2, 1])
        for n, off in enumerate((1, prev)):
            add_sib(cb, off)
            to_dir(cb)[n].start()
        combine(0, mine(cb, 0, 0))

        @pl.when(cb >= LAG)
        def _():
            finish(cb - LAG)

        arrived(sib_in.at[cb, 0], ps_rs.at[cb % 2, 2])
        add_sib(cb, 0)

        @pl.when(cb >= 1)
        def _():
            merge(cb - 1)
        return carry

    lax.fori_loop(0, n_cb, down_step, 0)
    merge(n_cb - 1)
    for cb in range(max(0, n_cb - LAG), n_cb):
        finish(cb)

    took(idx_all.at[others], meta_ss.at[0])
    took(gate_all.at[others], meta_ss.at[1])
    for n, ref in enumerate((xall.at[pl.ds(0, 2)], xall.at[4], xall.at[pl.ds(0, CHIPS)], far_in, far_in, far_in)):
        took(ref, out_ss.at[n])
    for n in range(min(STAGES, n_cb)):
        took(acc.at[pl.ds(staged(n, 0, 0), 2 * CHIPS), tok], ps_ss.at[n])
    for cb in range(n_cb):
        y_copy(cb).wait()


def solution(mesh):
    assert mesh.shape["ep"] == 2 * CHIPS

    def group_layer(tokens, topk_idx, topk_w, w_up, w_down, slot_expert):
        n_tok, d_model = tokens.shape
        n_top = topk_idx.shape[1]
        n_dev, n_slot = slot_expert.shape
        d_ff = w_up.shape[-1]
        bound = slot_bound(n_tok, n_top, n_dev, n_slot)
        cap = bound // 8 * 8
        odd, rows_s = bound - cap, round_up(n_slot, 16)
        kb_w, cb_w = 2 * LANES, 2 * LANES
        n_kb, n_cb = d_model // kb_w, d_model // cb_w
        d_mid = n_dev * bound
        rows_src = n_slot * cap + odd * rows_s
        n_acc = max(n_slot * (d_ff // LANES), (n_cb + STAGES) * CHIPS * 2)
        cfg = dict(bound=bound, cap=cap, kb_w=kb_w, cb_w=cb_w)
        dma = pltpu.SemaphoreType.DMA
        hbm = pl.BlockSpec(memory_space=pl.ANY)
        return pl.pallas_call(
            functools.partial(moe_kernel, cfg),
            out_shape=jax.ShapeDtypeStruct((n_tok, d_model), BF16),
            in_specs=[hbm] * 6,
            out_specs=hbm,
            scratch_shapes=[
                pltpu.VMEM((n_dev, n_kb, n_tok, kb_w), BF16),
                pltpu.VMEM((n_dev, n_top, n_tok), jnp.int32),
                pltpu.VMEM((n_dev, n_top, n_tok), F32),
                pltpu.VMEM((n_dev, n_slot), jnp.int32),
                pltpu.VMEM((n_slot * cap, LANES), F32),
                pltpu.VMEM((n_dev, rows_src, n_tok), BF16),
                pltpu.VMEM((n_dev, 3 * n_tok, rows_src), BF16),
                pltpu.VMEM((n_slot, d_mid, kb_w), BF16),
                pltpu.VMEM((odd, kb_w // LANES, rows_s * n_dev, LANES), F32),
                pltpu.VMEM((n_acc, max(d_mid, n_tok), LANES), F32),
                pltpu.VMEM((n_slot, d_mid, d_ff), BF16),
                pltpu.VMEM((n_dev, rows_src, cb_w), BF16),
                pltpu.VMEM((odd, cb_w // LANES, n_dev * rows_s, LANES), F32),
                pltpu.VMEM((n_slot, kb_w, d_ff), BF16),
                pltpu.VMEM((n_slot, d_ff, cb_w), BF16),
                pltpu.VMEM((n_cb, CHIPS, 2, n_tok, LANES), F32),
                pltpu.VMEM((n_cb, 2, n_tok, LANES), F32),
                pltpu.VMEM((n_cb, 4, n_tok, LANES), F32),
                pltpu.VMEM((n_cb, n_tok, cb_w), BF16),
                dma((4,)), dma((2,)), dma((2,)), dma((6,)),
                dma((n_kb,)), dma((n_kb,)), dma((n_kb,)),
                dma((-(-n_slot // GROUP),)), dma((-(-n_slot // GROUP),)),
                dma((STAGES,)), dma((2, 3)), dma((n_cb,)), dma((n_cb,)), dma((n_cb,)),
            ],
            compiler_params=pltpu.CompilerParams(collective_id=0, has_side_effects=True, vmem_limit_bytes=67_000_000),
        )(tokens, topk_idx.T, topk_w.T, slot_expert, w_up, w_down)

    row_spec = P(('dp', 'ep'), None)
    weight_spec = P('ep', None, None, None)
    return jax.shard_map(group_layer, mesh=mesh, in_specs=(row_spec, row_spec, row_spec, weight_spec, weight_spec, P(None, None)),
                         out_specs=row_spec, check_vma=False)
```

time: 107 us -> 106 us (level)
  no operation moved by 1% of the time
where the time goes in v5:
time: 106 us
  Pallas kernels  104 us (98%)
  local copies, waits for them, and re-layouts  2.09 us (2%)
    pallas_call x1, Pallas kernels, group_layer(): pl.pallas_call(functools.partial(moe_kernel, cfg), out_shape=jax.ShapeDty...  104 us

profile of v5, /device:TPU:81, one launch (start us, length us, event | category | flops | bytes accessed | tf_op | source)
XLA Modules:
  0.0 106.3 jit_solution(495039189835653829)
XLA Ops:
  0.0 104.2 %shard_map.64 = bf16[192,2048]{1,0:T(8,128)(2,1)} custom-call(bf16[192,2048]{1,0:T(8,128)(2,1)} %x_ref.1, s32[6,192]{1,0:T(8,128)} %bitcast.2, f32[6,192]{1,0:T(8,128)} %bitcast.3, s32[8,9]{1,0:T(8,128)} %tab_ref.1, bf16[1,9,2048,1408]{3,2,1,0:T(8,128)(2,1)} %wup_ref.1, bf16[1,9,1408,2048]{3,2,1,0:T(8,128)(2,1)} %wdn_ref.1), custom_call_target="tpu_custom_call" | custom-call | tf_op jit(solution)/shard_map/pallas_call | solution.py:409
  104.3 2.1 %copy.8 = bf16[192,2048]{1,0:T(8,128)(2,1)} copy(bf16[192,2048]{1,0:T(8,128)(2,1)} %shard_map.64) | data formatting | bytes 1572864
